TPU v7x, 256 devices: a whole 4x4x8 slice. The times are simulated.
256 devices in a mesh: row: 32 (over z, y_hi, core), col: 8 (over y_lo, x).
Axes of the slice: x: 4, y: 4 (y_hi: 2, y_lo: 2; y = y_hi * 2 + y_lo), z: 8, core: 2. Of those that a mesh axis runs over, the one named last changes fastest.
Arguments:
- inputs: bfloat16 [12288, 1024], P(('row', 'col')), may hold values from -24 to 24
- first_weight: bfloat16 [1024, 1024], replicated, may hold values from -0.1875 to 0.1875
- second_weight: bfloat16 [1024, 1024], replicated, may hold values from -0.1875 to 0.1875
- readout: bfloat16 [1024], replicated, may hold values from -0.1875 to 0.1875
- target: float32 [12288], P(('row', 'col')), may hold values from -6 to 6
- counts: int32 [12288], P(('row', 'col')), may hold values from 1 to 32, as said below
- views: int32 [12288], P(('row', 'col')), may hold values from 0 to 1999
Outputs:
- update: float32 [1024, 2048], P(('row', 'col'))
Inputs may be any that keep to these rules, and one draw needn't show every extreme that they name: `counts`: number of samples taken along the ray.
All inputs are finite; a program needn't handle non-finite values.
Results may differ from a plain program's by a relative error of at most 0.008.
Values may be sent and summed in bfloat16 or wider, within the bound.
A program may use at most 128 MiB of HBM per device.

v0:
```python
import functools

import jax
import jax.numpy as jnp
from jax import lax
from jax.sharding import Mesh
from jax.sharding import PartitionSpec as P

VIEWS = 2000
ITERS = 3
ROW_COL = ("row_0", "row_1", "row_2", "col_0", "col_1")
COL = ("col_0", "col_1")
ROW = ("row_0", "row_1", "row_2")


DAMP = 4.0
LEARN = 8.0
HIGH = lax.Precision.HIGHEST


def by_axis(shard, axes):
    return functools.reduce(lax.psum, axes, shard)


def in_one_piece(arrays, axis, dim, along):
    ends, at = ([], 0)
    for a in arrays[:-1]:
        at += a.shape[along]
        ends.append(at)
    both = jnp.concatenate(arrays, axis=along)
    return tuple(jnp.split(lax.all_gather(both, axis, axis=dim, tiled=True), ends, axis=along))


def from_everyone(shard, axis):
    copies = jnp.broadcast_to(shard, (lax.axis_size(axis), *shard.shape))
    return lax.all_to_all(copies, axis, split_axis=0, concat_axis=0, tiled=True)


def laid_out(parts, dim):
    lengths = list(parts.shape[1:])
    lengths[dim] *= parts.shape[0]
    return jnp.moveaxis(parts, 0, dim).reshape(lengths)


def collect(shard, axis, dim):
    parts = from_everyone(shard, axis)
    return laid_out(parts, dim)


def in_blocks(shard, dim, devices):
    before, after = (shard.shape[:dim], shard.shape[dim + 1 :])
    return jnp.moveaxis(shard.reshape(*before, devices, -1, *after), dim, 0)


def summed_on_arrival(shard, axis, dim):
    devices = lax.axis_size(axis)
    parts = lax.all_to_all(in_blocks(shard, dim, devices), axis, 0, 0, tiled=True)
    return jnp.sum(parts, axis=0)


def summed_on_arrival_2(shard, axis, dim):
    parts = in_blocks(shard, dim, lax.axis_size(axis))
    arrived = lax.all_to_all(parts, axis, split_axis=0, concat_axis=0, tiled=True)
    return arrived.astype(jnp.float32).sum(axis=0)


def slope(value):
    sig = jax.nn.sigmoid(value)
    return sig * (1.0 + value * (1.0 - sig))


def ray_weight(counts, views):
    angle = 2.0 * jnp.pi / VIEWS * views.astype(jnp.float32)
    return counts.astype(jnp.float32) / 16.0 * (1.0 + 0.5 * jnp.cos(angle))


def carry_back(outer_grad, second_weight, pre_first):
    carried = lax.dot_general(
        outer_grad, second_weight, (((1,), (1,)), ((), ())), preferred_element_type=jnp.float32
    )
    return (carried * slope(pre_first)).astype(jnp.bfloat16)


def gram(left, other):
    return lax.dot_general(
        left, other, (((1,), (1,)), ((), ())), preferred_element_type=jnp.float32
    )


def global_sums(values):
    return (by_axis(values[0], ROW_COL), by_axis(values[1], ROW_COL))


def shards(inputs, first_weight, second_weight, readout, target, counts, views):
    weight_rows = ray_weight(counts, views)
    pre_first = jnp.dot(inputs, first_weight, preferred_element_type=jnp.float32)
    hidden = jax.nn.silu(pre_first).astype(jnp.bfloat16)
    pre_second = jnp.dot(hidden, second_weight, preferred_element_type=jnp.float32)
    readout_f = readout.astype(jnp.float32)
    signal = jnp.sum(jax.nn.silu(pre_second) * readout_f[None, :], axis=1)
    right = weight_rows * signal - target
    outer_grad = (weight_rows[:, None] * slope(pre_second) * readout_f[None, :]).astype(
        jnp.bfloat16
    )
    inner_grad = carry_back(outer_grad, second_weight, pre_first)
    block_in, block_inner, block_hidden, block_outer = in_one_piece(
        (inputs, inner_grad, hidden, outer_grad), COL, 0, 1
    )
    cross_in, cross_hidden, cross_outer = in_one_piece((inputs, hidden, outer_grad), ROW, 0, 1)
    cross_pre = jnp.dot(cross_in, first_weight, preferred_element_type=jnp.float32)
    cross_inner = carry_back(cross_outer, second_weight, cross_pre)
    kernel = gram(block_in, cross_in) * gram(block_inner, cross_inner)
    kernel = kernel + gram(block_hidden, cross_hidden) * gram(block_outer, cross_outer)

    def apply(direction):
        spread = collect(direction, ROW, 0)
        partial_value = jnp.dot(kernel, spread, precision=HIGH, preferred_element_type=jnp.float32)
        own = summed_on_arrival(partial_value, COL, 0)
        return own + DAMP * direction

    solution = jnp.zeros_like(right)
    residual = right
    image = apply(residual)
    norm_now, product = global_sums((jnp.sum(residual * residual), jnp.sum(residual * image)))
    alpha = norm_now / product
    direction, along = (residual, image)
    for step in range(ITERS):
        solution = solution + alpha * direction
        residual = residual - alpha * along
        if step + 1 < ITERS:
            image = apply(residual)
            norm_next, product = global_sums(
                (jnp.sum(residual * residual), jnp.sum(residual * image))
            )
            ratio = norm_next / norm_now
            alpha = norm_next / (product - ratio * norm_next / alpha)
            direction = residual + ratio * direction
            along = image + ratio * along
            norm_now = norm_next
    block_solution = collect(solution, COL, 0)
    width = inner_grad.shape[1] // lax.axis_size(COL)
    first_column = lax.axis_index(COL) * width
    sel_inner = (
        lax.dynamic_slice_in_dim(block_inner, first_column, width, 1).astype(jnp.float32)
        * block_solution[:, None]
    )
    sel_outer = (
        lax.dynamic_slice_in_dim(block_outer, first_column, width, 1).astype(jnp.float32)
        * block_solution[:, None]
    )
    block_in_f = block_in.astype(jnp.float32)
    block_hid_f = block_hidden.astype(jnp.float32)
    first = lax.dot_general(
        block_in_f,
        sel_inner,
        (((0,), (0,)), ((), ())),
        precision=HIGH,
        preferred_element_type=jnp.float32,
    )
    second = lax.dot_general(
        block_hid_f,
        sel_outer,
        (((0,), (0,)), ((), ())),
        precision=HIGH,
        preferred_element_type=jnp.float32,
    )
    share = summed_on_arrival_2(
        (-LEARN * jnp.stack([first, second], axis=1)).astype(jnp.bfloat16), ROW, 0
    )
    placed = lax.all_to_all(
        share.astype(jnp.bfloat16), COL, split_axis=0, concat_axis=2, tiled=True
    ).astype(share.dtype)
    return placed.reshape(placed.shape[0], 2 * inputs.shape[1])


def solution(mesh):
    split = Mesh(mesh.devices.reshape(8, 2, 2, 2, 4), ("row_0", "row_1", "row_2", "col_0", "col_1"))
    in_specs = (P(ROW_COL, None), P(), P(), P(), P(ROW_COL), P(ROW_COL), P(ROW_COL))
    out_specs = P(ROW_COL, None)
    return jax.shard_map(
        shards, mesh=split, in_specs=in_specs, out_specs=out_specs, check_vma=False
    )
```

profile of v0, /device:TPU:1, one launch (start us, length us, event | category | flops | bytes accessed | tf_op | source)
XLA Modules:
  0.0 463.7 jit_solution(15295629557523191135)
XLA Ops:
  14.4 22.0 %all_to_all.65 = f32[32,1,48]{2,1,0:T(1,128)S(1)} all-to-all(f32[32,1,48]{2,1,0:T(1,128)S(1)} %broadcast_in_dim.15), channel_id=1, replica_groups=mesh['row_0'=8,'row_1'=2,'row_2'=2,'col_0'=2,'col_1'=4] {'row_0','row_1'..., dimensions={0} | all-to-all | bytes 12288 | tf_op jit(solution)/shard_map/all_to_all | solution.py:36
  37.6 23.8 %all-gather.3.cloned.1.call-done = bf16[384,4096]{1,0:T(8,128)(2,1)} async-done(((bf16[48,4096]{1,0:T(8,128)(2,1)}), bf16[384,4096]{1,0:T(8,128)(2,1)}) %all-gather.3.cloned.1.call-update) | async-done | bytes 3145744 | tf_op jit(solution)/shard_map/all_gather | solution.py:31
  61.4 110.4 %all-gather.5.cloned.1.call-done = bf16[1536,3072]{1,0:T(8,128)(2,1)} async-done(((bf16[48,3072]{1,0:T(8,128)(2,1)}), bf16[1536,3072]{1,0:T(8,128)(2,1)}) %all-gather.5.cloned.1.call-update) | async-done | bytes 9437200 | tf_op jit(solution)/shard_map/all_gather | solution.py:31
  171.8 3.7 fusion.6
  175.6 5.5 %fusion.11 = f32[384,1536]{1,0:T(8,128)} fusion(bf16[1536,3072]{1,0:T(8,128)(2,1)} %all-gather.5.cloned.1.call-done, bf16[384,4096]{1,0:T(8,128)(2,1)S(1)} %copy-done.2), kind=kOutput, calls=%fused_computation.11 | convolution fusion | flops 1207959552 | bytes 6291456 | tf_op jit(solution)/shard_map/dot_general | solution.py:85
  181.1 5.3 %fusion.9 = f32[1536,1024]{1,0:T(8,128)} fusion(bf16[1024,1024]{1,0:T(8,128)(2,1)S(1)} %copy-done, bf16[1536,3072]{1,0:T(8,128)(2,1)S(1)} %bitcast.44), kind=kOutput, calls=%fused_computation.9 | convolution fusion | flops 3221225472 | bytes 11534336 | tf_op jit(solution)/shard_map/dot_general | solution.py:110
  189.3 12.7 %fusion.5 = f32[384,1536]{1,0:T(8,128)} fusion(f32[384,1536]{1,0:T(8,128)} %fusion.2, f32[384,1536]{1,0:T(8,128)} %fusion.11, f32[1536,1024]{1,0:T(8,128)} %fusion.9, bf16[1024,1024]{1,0:T(8,128)(2,1)} %param.9, bf16[1536,3072]{1,0:T(8,128)(2,1)} %all-gather.5.cloned.1.call-done, bf16[384,4096]{1,0:T(8,128)(2,1)} %all-gather.3.cloned.1.call-done), kind=kOutput, calls=%fused_computation.5 | convolution fusion | flops 4444520448 | bytes 19398656 | tf_op jit(solution)/shard_map/dot_general | solution.py:85
  202.1 5.1 %convolution_bitcast_fusion.2 = f32[8,1,48]{2,1,0:T(1,128)S(1)} fusion(f32[8,48,1536]{2,1,0:T(8,128)} %bitcast.38, f32[1536,1,1]{0,1,2:T(1,128)S(1)} %reshape.60), kind=kOutput, calls=%fused_computation.17 | convolution fusion | flops 7077888 | bytes 2366976 | tf_op jit(solution)/shard_map/dot_general | solution.py:117
  207.2 8.8 %all_to_all.66 = f32[8,1,48]{2,1,0:T(1,128)S(1)} all-to-all(f32[8,1,48]{2,1,0:T(1,128)S(1)} %convolution_bitcast_fusion.2), channel_id=1, replica_groups=mesh['row_0'=8,'row_1'=2,'row_2'=2,'col_0'=2,'col_1'=4] {'col_0','col_1'}, dimensions={0} | all-to-all | bytes 3072 | tf_op jit(solution)/shard_map/all_to_all | solution.py:57
  216.6 13.2 %all-reduce.2 = (f32[]{:T(128)}, f32[]{:T(128)}) all-reduce(f32[]{:T(128)} %get-tuple-element.10, f32[]{:T(128)} %get-tuple-element.9), channel_id=1, replica_groups=mesh['row_0'=8,'row_1'=2,'row_2'=2,'col_0'=2,'col_1'=4] {'row_0'}, use_global_device_ids=true, to_apply=%region_2.3 | all-reduce | flops 2 | bytes 16 | tf_op jit(solution)/shard_map/psum | solution.py:22
  229.8 5.9 %all-reduce.14 = (f32[]{:T(128)}, f32[]{:T(128)}) all-reduce(f32[]{:T(128)} %get-tuple-element.15, f32[]{:T(128)} %get-tuple-element.16), channel_id=1, replica_groups=mesh['row_0'=8,'row_1'=2,'row_2'=2,'col_0'=2,'col_1'=4] {'row_1'}, use_global_device_ids=true, to_apply=%region_3.4 | all-reduce | flops 2 | bytes 16 | tf_op jit(solution)/shard_map/psum | solution.py:22
  235.7 9.4 %all-reduce.11 = (f32[]{:T(128)}, f32[]{:T(128)}) all-reduce(f32[]{:T(128)} %get-tuple-element.39, f32[]{:T(128)} %get-tuple-element.40), channel_id=1, replica_groups=mesh['row_0'=8,'row_1'=2,'row_2'=2,'col_0'=2,'col_1'=4] {'row_2'}, use_global_device_ids=true, to_apply=%region_4.5 | all-reduce | flops 2 | bytes 16 | tf_op jit(solution)/shard_map/psum | solution.py:22
  245.1 4.4 all-reduce.8
  249.5 7.5 %all-reduce.5 = (f32[]{:T(128)}, f32[]{:T(128)}) all-reduce(f32[]{:T(128)} %get-tuple-element.27, f32[]{:T(128)} %get-tuple-element.28), channel_id=1, replica_groups=mesh['row_0'=8,'row_1'=2,'row_2'=2,'col_0'=2,'col_1'=4] {'col_1'}, use_global_device_ids=true, to_apply=%region_6.7 | all-reduce | flops 2 | bytes 16 | tf_op jit(solution)/shard_map/psum | solution.py:22
  258.3 18.8 %all_to_all.67 = f32[32,1,48]{2,1,0:T(1,128)S(1)} all-to-all(f32[32,1,48]{2,1,0:T(1,128)S(1)} %broadcast_in_dim.16), channel_id=1, replica_groups=mesh['row_0'=8,'row_1'=2,'row_2'=2,'col_0'=2,'col_1'=4] {'row_0','row_1'..., dimensions={0} | all-to-all | bytes 12288 | tf_op jit(solution)/shard_map/all_to_all | solution.py:36
  277.8 5.1 %convolution_bitcast_fusion.1 = f32[8,1,48]{2,1,0:T(1,128)S(1)} fusion(f32[8,48,1536]{2,1,0:T(8,128)} %bitcast.39, f32[1536,1,1]{0,1,2:T(1,128)S(1)} %reshape.62), kind=kOutput, calls=%fused_computation.16 | convolution fusion | flops 7077888 | bytes 2366976 | tf_op jit(solution)/shard_map/dot_general | solution.py:117
  282.9 7.4 %all_to_all.68 = f32[8,1,48]{2,1,0:T(1,128)S(1)} all-to-all(f32[8,1,48]{2,1,0:T(1,128)S(1)} %convolution_bitcast_fusion.1), channel_id=1, replica_groups=mesh['row_0'=8,'row_1'=2,'row_2'=2,'col_0'=2,'col_1'=4] {'col_0','col_1'}, dimensions={0} | all-to-all | bytes 3072 | tf_op jit(solution)/shard_map/all_to_all | solution.py:57
  291.0 11.6 %all-reduce.1 = (f32[]{:T(128)}, f32[]{:T(128)}) all-reduce(f32[]{:T(128)} %get-tuple-element.8, f32[]{:T(128)} %get-tuple-element.7), channel_id=1, replica_groups=mesh['row_0'=8,'row_1'=2,'row_2'=2,'col_0'=2,'col_1'=4] {'row_0'}, use_global_device_ids=true, to_apply=%region_15.16 | all-reduce | flops 2 | bytes 16 | tf_op jit(solution)/shard_map/psum | solution.py:22
  302.6 5.9 %all-reduce.13 = (f32[]{:T(128)}, f32[]{:T(128)}) all-reduce(f32[]{:T(128)} %get-tuple-element.13, f32[]{:T(128)} %get-tuple-element.14), channel_id=1, replica_groups=mesh['row_0'=8,'row_1'=2,'row_2'=2,'col_0'=2,'col_1'=4] {'row_1'}, use_global_device_ids=true, to_apply=%region_16.17 | all-reduce | flops 2 | bytes 16 | tf_op jit(solution)/shard_map/psum | solution.py:22
  308.5 9.5 %all-reduce.10 = (f32[]{:T(128)}, f32[]{:T(128)}) all-reduce(f32[]{:T(128)} %get-tuple-element.37, f32[]{:T(128)} %get-tuple-element.38), channel_id=1, replica_groups=mesh['row_0'=8,'row_1'=2,'row_2'=2,'col_0'=2,'col_1'=4] {'row_2'}, use_global_device_ids=true, to_apply=%region_17.18 | all-reduce | flops 2 | bytes 16 | tf_op jit(solution)/shard_map/psum | solution.py:22
  318.0 4.4 all-reduce.7
  322.4 7.5 %all-reduce.4 = (f32[]{:T(128)}, f32[]{:T(128)}) all-reduce(f32[]{:T(128)} %get-tuple-element.25, f32[]{:T(128)} %get-tuple-element.26), channel_id=1, replica_groups=mesh['row_0'=8,'row_1'=2,'row_2'=2,'col_0'=2,'col_1'=4] {'col_1'}, use_global_device_ids=true, to_apply=%region_19.20 | all-reduce | flops 2 | bytes 16 | tf_op jit(solution)/shard_map/psum | solution.py:22
  334.2 16.9 %all_to_all.69 = f32[32,1,48]{2,1,0:T(1,128)S(1)} all-to-all(f32[32,1,48]{2,1,0:T(1,128)S(1)} %broadcast_in_dim.17), channel_id=1, replica_groups=mesh['row_0'=8,'row_1'=2,'row_2'=2,'col_0'=2,'col_1'=4] {'row_0','row_1'..., dimensions={0} | all-to-all | bytes 12288 | tf_op jit(solution)/shard_map/all_to_all | solution.py:36
  351.8 5.7 %convolution_bitcast_fusion = f32[8,1,48]{2,1,0:T(1,128)} fusion(f32[8,48,1536]{2,1,0:T(8,128)} %bitcast.40, f32[1536,1,1]{0,1,2:T(1,128)S(1)} %reshape.64), kind=kOutput, calls=%fused_computation.15 | convolution fusion | flops 7077888 | bytes 2366976 | tf_op jit(solution)/shard_map/dot_general | solution.py:117
  360.9 4.9 %all-to-all-done.5 = f32[8,1,48]{2,1,0:T(1,128)S(1)} async-done(((f32[8,1,48]{2,1,0:T(1,128)}), f32[8,1,48]{2,1,0:T(1,128)S(1)}, u32[]{:S(2)}, u32[]{:S(2)}) %all-to-all-start.5) | async-done | bytes 1568 | tf_op jit(solution)/shard_map/all_to_all | solution.py:57
  366.4 11.6 %all-reduce = (f32[]{:T(128)}, f32[]{:T(128)}) all-reduce(f32[]{:T(128)} %get-tuple-element.6, f32[]{:T(128)} %get-tuple-element.5), channel_id=1, replica_groups=mesh['row_0'=8,'row_1'=2,'row_2'=2,'col_0'=2,'col_1'=4] {'row_0'}, use_global_device_ids=true, to_apply=%region_28.29 | all-reduce | flops 2 | bytes 16 | tf_op jit(solution)/shard_map/psum | solution.py:22
  378.0 5.9 %all-reduce.12 = (f32[]{:T(128)}, f32[]{:T(128)}) all-reduce(f32[]{:T(128)} %get-tuple-element.11, f32[]{:T(128)} %get-tuple-element.12), channel_id=1, replica_groups=mesh['row_0'=8,'row_1'=2,'row_2'=2,'col_0'=2,'col_1'=4] {'row_1'}, use_global_device_ids=true, to_apply=%region_29.30 | all-reduce | flops 2 | bytes 16 | tf_op jit(solution)/shard_map/psum | solution.py:22
  383.9 9.5 %all-reduce.9 = (f32[]{:T(128)}, f32[]{:T(128)}) all-reduce(f32[]{:T(128)} %get-tuple-element.35, f32[]{:T(128)} %get-tuple-element.36), channel_id=1, replica_groups=mesh['row_0'=8,'row_1'=2,'row_2'=2,'col_0'=2,'col_1'=4] {'row_2'}, use_global_device_ids=true, to_apply=%region_30.31 | all-reduce | flops 2 | bytes 16 | tf_op jit(solution)/shard_map/psum | solution.py:22
  393.4 4.4 all-reduce.6
  397.8 7.5 %all-reduce.3 = (f32[]{:T(128)}, f32[]{:T(128)}) all-reduce(f32[]{:T(128)} %get-tuple-element.23, f32[]{:T(128)} %get-tuple-element.24), channel_id=1, replica_groups=mesh['row_0'=8,'row_1'=2,'row_2'=2,'col_0'=2,'col_1'=4] {'col_1'}, use_global_device_ids=true, to_apply=%region_32.33 | all-reduce | flops 2 | bytes 16 | tf_op jit(solution)/shard_map/psum | solution.py:22
  423.2 25.5 %all_to_all.70 = bf16[32,32,2,128]{3,1,2,0:T(8,128)(2,1)S(1)} all-to-all(bf16[32,32,2,128]{3,1,2,0:T(8,128)(2,1)S(1)} %fusion.16), channel_id=1, replica_groups=mesh['row_0'=8,'row_1'=2,'row_2'=2,'col_0'=2,'col_1'=4] {'row_0','row_1'..., dimensions={0} | all-to-all | bytes 1048576 | tf_op jit(solution)/shard_map/all_to_all | solution.py:63
  448.8 7.4 %all_to_all.71 = bf16[32,2,128]{2,1,0:T(2,128)(2,1)S(1)} all-to-all(bf16[32,2,128]{2,1,0:T(2,128)(2,1)S(1)} %copy.13), channel_id=1, replica_groups=mesh['row_0'=8,'row_1'=2,'row_2'=2,'col_0'=2,'col_1'=4] {'col_0','col_1'}, dimensions={0} | all-to-all | bytes 32768 | tf_op jit(solution)/shard_map/all_to_all | solution.py:170
  (67 shorter events, 33.2 us)
Async XLA Ops:
  6.5 1.6 copy-start
  6.5 5.3 %copy-start.4 = (f32[48]{0:T(128)S(1)}, f32[48]{0:T(128)}, u32[]{:S(2)}) copy-start(f32[48]{0:T(128)} %param.11) | copy-start | bytes 580
  6.5 5.3 %copy-start.6 = (s32[48]{0:T(128)S(1)}, s32[48]{0:T(128)}, u32[]{:S(2)}) copy-start(s32[48]{0:T(128)} %param.12) | copy-start | bytes 580
  6.5 5.3 %copy-start.5 = (s32[48]{0:T(128)S(1)}, s32[48]{0:T(128)}, u32[]{:S(2)}) copy-start(s32[48]{0:T(128)} %param.13) | copy-start | bytes 580
  6.5 54.8 %all-gather.3.cloned.1.call-start = ((), (), s32[]{:S(2)}) async-start(), calls=%async_computation.9 | async-start | bytes 3538944 | tf_op jit(solution)/shard_map/all_gather | solution.py:31
  6.6 5.4 %copy-start.1 = (bf16[1024,1024]{1,0:T(8,128)(2,1)S(1)}, bf16[1024,1024]{1,0:T(8,128)(2,1)}, u32[]{:S(2)}) copy-start(bf16[1024,1024]{1,0:T(8,128)(2,1)} %param.9) | copy-start | bytes 6291460
  9.5 3.2 copy-start.3
  13.5 158.3 %all-gather.5.cloned.1.call-start = ((), (), s32[]{:S(2)}) async-start(), calls=%async_computation.10 | async-start | bytes 9732096 | tf_op jit(solution)/shard_map/all_gather | solution.py:31
  171.8 3.7 copy-start.2
  171.8 9.3 %slice-start = ((s8[9437184]{0:T(1024)(128)(4,1)}), s8[4194304]{0:T(1024)(128)(4,1)S(1)}, s32[]{:S(2)}) async-start(s8[9437184]{0:T(1024)(128)(4,1)} %bitcast.43), calls=%async_computation.11 | async-start | bytes 8388608
  171.8 9.3 %slice-start.1 = ((s8[9437184]{0:T(1024)(128)(4,1)}), s8[4194304]{0:T(1024)(128)(4,1)S(1)}, s32[]{:S(2)}) async-start(s8[9437184]{0:T(1024)(128)(4,1)} %bitcast.43), calls=%async_computation.12 | async-start | bytes 8388608
  175.6 5.6 %slice-start.2 = ((s8[9437184]{0:T(1024)(128)(4,1)}), s8[1048576]{0:T(1024)(128)(4,1)S(1)}, s32[]{:S(2)}) async-start(s8[9437184]{0:T(1024)(128)(4,1)} %bitcast.43), calls=%async_computation.13 | async-start | bytes 2097152
  357.6 8.2 %all-to-all-start.5 = ((f32[8,1,48]{2,1,0:T(1,128)}), f32[8,1,48]{2,1,0:T(1,128)S(1)}, u32[]{:S(2)}, u32[]{:S(2)}) async-start(f32[8,1,48]{2,1,0:T(1,128)} %convolution_bitcast_fusion), calls=%async_computation.5 | async-start | bytes 8192 | tf_op jit(solution)/shard_map/all_to_all | solution.py:57
  409.7 8.2 %all-to-all-start.6 = ((f32[8,1,48]{2,1,0:T(1,128)}), f32[8,1,48]{2,1,0:T(1,128)S(1)}, u32[]{:S(2)}, u32[]{:S(2)}) async-start(f32[8,1,48]{2,1,0:T(1,128)} %broadcast_in_dim.18), calls=%async_computation.6 | async-start | bytes 8192 | tf_op jit(solution)/shard_map/all_to_all | solution.py:36
Sparse Core Ops, SparseCore 0:
  13.7 47.6 all-gather.2
  64.2 107.6 all-gather.4
where the time goes:
time: 466 us; the launch traced here: 464 us
  blocking collectives  225 us (48%)
  waiting for transfers between devices  142 us (30%)
  matrix products  54.9 us (12%)
  between operations  23.1 us (5%)
  other arithmetic  7.64 us (2%)
  starting transfers between devices  6.69 us (1%)
    all_gather x2, waiting for transfers between devices, in_one_piece(): lax.all_gather(both, axis, axis=dim, tiled=True)  134 us
    psum x15, blocking collectives, by_axis(): return functools.reduce(lax.psum, axes, shard)  118 us
    all_to_all x3, blocking collectives, from_everyone(): return lax.all_to_all(copies, axis, split_axis=0, concat_axis=0, tiled=True)  57.7 us
    all_to_all x1, blocking collectives, summed_on_arrival_2(): lax.all_to_all(parts, axis, split_axis=0, concat_axis=0, tiled=True)  25.5 us
    dot_general x4, matrix products, gram(): lax.dot_general(left, other, (((1,), (1,)), ((), ())), preferred_element_...  24.9 us
    all_to_all x2, blocking collectives, summed_on_arrival(): lax.all_to_all(in_blocks(shard, dim, devices), axis, 0, 0, tiled=True)  16.2 us
    dot_general x3, matrix products, apply(): jnp.dot(kernel, spread, precision=HIGH, preferred_element_type=jnp.float32)  15.9 us
  transfers between devices with their start and end apart: 4, of which 4 were waited for; matrix products, arithmetic and copies ran while one was open for 1% of the time, Pallas kernels for 0%

commit v1 on v0

v1 whole, which is shorter than its diff:
```python
import functools

import jax
import jax.numpy as jnp
from jax import lax
from jax.experimental import pallas as pl
from jax.experimental.pallas import tpu as pltpu
from jax.sharding import Mesh
from jax.sharding import PartitionSpec as P

VIEWS = 2000
DAMP = 4.0
LEARN = 8.0
AXES = ("z", "yh", "core", "yl", "x")
MESH = pl.DeviceIdType.MESH
F32 = jnp.float32
BF16 = jnp.bfloat16
CHUNK = 48
HALF = 384
SET = 768
WIDE = 256
NT = (((1,), (1,)), ((), ()))


def dot(a, b):
    return jnp.dot(a, b, preferred_element_type=F32)


def dot_nt(a, b):
    return lax.dot_general(a, b, NT, preferred_element_type=F32)


def sigmoid(value):
    return 0.5 * jnp.tanh(0.5 * value) + 0.5


def twice(column):
    return jnp.concatenate([column, column], axis=1)


def total_of(value):
    return jnp.sum(jnp.sum(value, axis=1, keepdims=True), axis=0, keepdims=True)


def step_kernel(
    x_hbm, w1_hbm, w2_hbm, side_ref, readout_ref, out_ref,
    w1, w2, xpa, xpb, hp, op, ip, xl, hl, ol, il, slope1, kern,
    side_p, side_l, side_rows, wcol_p, tcol_p, wcol_l, tcol_l, sig,
    half_r, x_t, h_t, plane_buf, line_buf, out_send, out_recv,
    load_sem, a_send, a_recv, b_send, b_recv, z_send, z_recv,
    core_send, core_recv, sp_sems, sl_sems, plane_sems, line_sems, out_sems,
):
    z, yh, c, yl, x = (lax.axis_index(name) for name in AXES)
    y = yh * 2 + yl
    me_p = y * 4 + x
    me_l = c * 8 + z

    def at(xx=None, yy=None, zz=None, cc=None):
        xx = x if xx is None else lax.rem(xx, 4)
        yy = y if yy is None else lax.rem(yy, 4)
        zz = z if zz is None else lax.rem(zz, 8)
        cc = c if cc is None else cc
        return (zz, yy // 2, cc, lax.rem(yy, 2), xx)

    plane_peers = [at(xx=x + k % 4, yy=y + k // 4) for k in range(1, 16)]
    line_same = [at(zz=z + k) for k in range(1, 8)]
    line_peers = line_same + [at(zz=z + k, cc=1 - c) for k in range(8)]

    def send(src, dst, ssem, rsem, dev):
        copy = pltpu.make_async_remote_copy(
            src_ref=src, dst_ref=dst, send_sem=ssem, recv_sem=rsem,
            device_id=dev, device_id_type=MESH,
        )
        copy.start()
        return copy

    def rows(slot, count=1):
        return pl.ds(pl.multiple_of(slot * CHUNK, CHUNK), count * CHUNK)

    loads = [
        pltpu.make_async_copy(x_hbm.at[:, pl.ds(0, 512)], xpa.at[rows(me_p)], load_sem.at[0]),
        pltpu.make_async_copy(x_hbm.at[:, pl.ds(512, 512)], xpb.at[rows(me_p)], load_sem.at[1]),
        pltpu.make_async_copy(x_hbm, xl.at[c, rows(z)], load_sem.at[2]),
        pltpu.make_async_copy(w1_hbm, w1, load_sem.at[3]),
        pltpu.make_async_copy(w2_hbm, w2, load_sem.at[4]),
    ]
    for load in loads:
        load.start()

    barrier = pltpu.get_barrier_semaphore()
    for peer in plane_peers + line_peers:
        pl.semaphore_signal(barrier, inc=1, device_id=peer, device_id_type=MESH)
    pl.semaphore_wait(barrier, 30)
    for load in loads[:3]:
        load.wait()

    xn, xq = at(xx=x + 1), at(xx=x + 3)
    yn, yq = at(yy=y + 1), at(yy=y + 3)
    zn, zq = at(zz=z + 1), at(zz=z + 7)
    xm1, xp1 = lax.rem(x + 3, 4), lax.rem(x + 1, 4)
    ym1, yp1 = lax.rem(y + 3, 4), lax.rem(y + 1, 4)
    pending = []

    def pa(yy, xx):
        return rows(yy * 4 + xx)

    def go(ref, index, ssem, rsem, k, dev):
        copy = send(ref.at[index], ref.at[index], ssem.at[k], rsem.at[k], dev)
        pending.append(copy)
        return copy

    own = rows(me_p)
    a1 = [go(xpa, (own,), a_send, a_recv, 0, xn), go(xpa, (own,), a_send, a_recv, 1, xq)]
    b1 = [go(xpb, (own,), b_send, b_recv, 0, yn), go(xpb, (own,), b_send, b_recv, 1, yq)]
    z1 = [
        go(xl, (c, rows(z)), z_send, z_recv, 0, zn),
        go(xl, (c, rows(z)), z_send, z_recv, 1, zq),
    ]
    for k in range(15):
        send(side_ref, side_p.at[me_p], sp_sems.at[0], sp_sems.at[1], plane_peers[k])
    for k in range(7):
        send(side_ref, side_l.at[z], sl_sems.at[0], sl_sems.at[1], line_same[k])
    side_p[me_p] = side_ref[...]
    side_l[z] = side_ref[...]

    low, high = pl.ds(0, 256), pl.ds(256, 256)
    a1[0].wait_recv()
    a2 = [go(xpa, (pa(y, xm1), low), a_send, a_recv, 2, xn)]
    a1[1].wait_recv()
    a2 += [go(xpa, (pa(y, xp1), high), a_send, a_recv, 3, xq)]
    b1[0].wait_recv()
    b2 = [go(xpb, (pa(ym1, x), low), b_send, b_recv, 2, yn)]
    b1[1].wait_recv()
    b2 += [go(xpb, (pa(yp1, x), high), b_send, b_recv, 3, yq)]

    def ring(step, before):
        down, up = lax.rem(z + 8 - step, 8), lax.rem(z + step, 8)
        lanes = (slice(None), slice(None)) if step < 3 else (pl.ds(0, 512), pl.ds(512, 512))
        before[0].wait_recv()
        one = go(xl, (c, rows(down), lanes[0]), z_send, z_recv, 2 * step, zn)
        before[1].wait_recv()
        two = go(xl, (c, rows(up), lanes[1]), z_send, z_recv, 2 * step + 1, zq)
        return [one, two]

    z2 = ring(1, z1)
    for copy in a2:
        copy.wait_recv()
    line_y = (rows(y * 4, 4),)
    a3 = [go(xpa, line_y, a_send, a_recv, 4, yn), go(xpa, line_y, a_send, a_recv, 5, yq)]
    for copy in b2:
        copy.wait_recv()
    b3 = []
    for side, dev in ((0, xn), (1, xq)):
        b3.append([go(xpb, (pa(yy, x),), b_send, b_recv, 4 + 4 * side + yy, dev) for yy in range(4)])
    z3 = ring(2, z2)
    a3[0].wait_recv()
    a4 = [go(xpa, (rows(ym1 * 4, 2),), a_send, a_recv, 6, yn)]
    a3[1].wait_recv()
    a4 += [go(xpa, (rows(yp1 * 4 + 2, 2),), a_send, a_recv, 7, yq)]
    b4 = []
    for copy in b3[0]:
        copy.wait_recv()
    b4 += [go(xpb, (pa(yy, xm1),), b_send, b_recv, 12 + yy, xn) for yy in range(2)]
    for copy in b3[1]:
        copy.wait_recv()
    b4 += [go(xpb, (pa(yy, xp1),), b_send, b_recv, 12 + yy, xq) for yy in range(2, 4)]
    z4 = ring(3, z3)

    def many(ref, count, sems, which):
        view = ref.at[pl.ds(0, count)]
        pltpu.make_async_copy(view, view, sems.at[which]).wait()

    many(side_p, 15, sp_sems, 1)
    many(side_l, 7, sl_sems, 1)
    side_rows[...] = jnp.zeros_like(side_rows)
    side_rows[0:16, :] = side_p[:, 0, :]
    side_rows[16:32, :] = side_p[:, 1, :]
    side_rows[32:40, :] = side_l[:, 0, :]
    side_rows[40:48, :] = side_l[:, 1, :]
    turned = side_rows[...].T
    for s in range(16):
        place = pl.ds(s * CHUNK, CHUNK)
        wcol_p[place, :] = jnp.broadcast_to(turned[0:CHUNK, s : s + 1], (CHUNK, 128))
        tcol_p[place, :] = jnp.broadcast_to(turned[0:CHUNK, 16 + s : 17 + s], (CHUNK, 128))
    for s in range(8):
        place = pl.ds(s * CHUNK, CHUNK)
        wcol_l[place, :] = jnp.broadcast_to(turned[0:CHUNK, 32 + s : 33 + s], (CHUNK, 128))
        tcol_l[place, :] = jnp.broadcast_to(turned[0:CHUNK, 40 + s : 41 + s], (CHUNK, 128))
    loads[3].wait()
    loads[4].wait()

    def wide(n):
        return pl.ds(pl.multiple_of(n * WIDE, WIDE), WIDE)

    def forward(x_parts, h_ref, o_ref, i_ref, wcol, tcol, after):
        def first(n, carry):
            pre = sum(dot(part[...], w1[lo : lo + size, wide(n)]) for part, lo, size in x_parts)
            s = sigmoid(pre)
            h_ref[:, wide(n)] = (pre * s).astype(BF16)
            slope1[:, wide(n)] = s * (1.0 + pre * (1.0 - s))
            return carry

        lax.fori_loop(0, 4, first, 0)
        after(0)
        sig[...] = jnp.zeros_like(sig)

        def second(n, carry):
            pre = dot(h_ref[...], w2[:, wide(n)])
            s = sigmoid(pre)
            gain = readout_ref[0:1, wide(n)]
            parts = pre * s * gain
            sig[...] += parts[:, 0:128] + parts[:, 128:256]
            o_ref[:, wide(n)] = (twice(wcol[...]) * (s * (1.0 + pre * (1.0 - s))) * gain).astype(BF16)
            return carry

        lax.fori_loop(0, 4, second, 0)
        after(1)

        def third(n, carry):
            back = dot_nt(o_ref[...], w2[wide(n), :])
            i_ref[:, wide(n)] = (back * slope1[:, wide(n)]).astype(BF16)
            return carry

        lax.fori_loop(0, 4, third, 0)
        after(2)
        lane = lax.broadcasted_iota(jnp.int32, (128, 128), 1)
        found = []
        for b in range(3):
            place = pl.ds(b * 128, 128)
            term = sig[place, :] * wcol[place, :] - jnp.where(lane == 0, tcol[place, :], 0.0)
            found.append(jnp.sum(term.T, axis=0, keepdims=True))
        return found

    sub = lax.broadcasted_iota(jnp.int32, (8, 128), 0)

    def packed(lines, first=0):
        value = jnp.zeros((8, 128), F32)
        for k, line in enumerate(lines):
            value = jnp.where(sub == first + k, line, value)
        return value

    for copy in z4:
        copy.wait_recv()
    partner = at(cc=1 - c)
    core_copies = [send(xl.at[c], xl.at[c], core_send.at[0], core_recv.at[0], partner)]

    def share(k):
        ref = (hl, ol, il)[k]
        core_copies.append(send(ref.at[c], ref.at[c], core_send.at[1 + k], core_recv.at[1 + k], partner))

    found = forward([(xl.at[c], 0, 1024)], hl.at[c], ol.at[c], il.at[c], wcol_l, tcol_l, share)
    half_r[c] = packed(found, c * 3)
    core_copies.append(send(half_r.at[c], half_r.at[c], core_send.at[4], core_recv.at[4], partner))

    for copy in a4 + b4:
        copy.wait_recv()
    found = []
    for b in range(2):
        place = pl.ds(b * HALF, HALF)
        found += forward(
            [(xpa.at[place], 0, 512), (xpb.at[place], 512, 512)],
            hp.at[place], op.at[place], ip.at[place], wcol_p.at[place], tcol_p.at[place],
            lambda k: None,
        )
    r0p = packed(found)

    def gram(which):
        def block(n, carry):
            place = wide(n)
            one = dot_nt(xl[which, :, 0:512], xpa[place, :]) + dot_nt(xl[which, :, 512:1024], xpb[place, :])
            value = one * dot_nt(il[which], ip[place, :])
            value = value + dot_nt(hl[which], hp[place, :]) * dot_nt(ol[which], op[place, :])
            kern[which, :, place] = value
            return carry

        lax.fori_loop(0, 3, block, 0)

    gram(c)
    for copy in core_copies:
        copy.wait_recv()
    r0l = half_r[0] + half_r[1]
    gram(1 - c)

    def products(dp, dl):
        lines_l, sums = [], [None] * 6
        for b in range(6):
            part = kern.at[b // 3, pl.ds((b % 3) * 128, 128)]
            if dl is not None:
                col = jnp.broadcast_to(dl[b : b + 1, :], (128, 128)).T
            acc = None
            for t in range(6):
                tile = part[:, t * 128 : (t + 1) * 128]
                term = tile * dp[t : t + 1, :]
                acc = term if acc is None else acc + term
                if dl is not None:
                    down = jnp.sum((tile * col).reshape(16, 8, 128), axis=0)
                    sums[t] = down if sums[t] is None else sums[t] + down
            lines_l.append(jnp.sum(acc.T, axis=0, keepdims=True))
        lines_p = [jnp.sum(s, axis=0, keepdims=True) for s in sums] if dl is not None else []
        return lines_p, packed(lines_l)

    def start_plane(k, value):
        plane_buf[k, me_p] = value
        for peer in plane_peers:
            send(plane_buf.at[k, me_p], plane_buf.at[k, me_p], plane_sems.at[k, 0], plane_sems.at[k, 1], peer)

    def start_line(k, value):
        line_buf[k, me_l] = value
        for peer in line_peers:
            send(line_buf.at[k, me_l], line_buf.at[k, me_l], line_sems.at[k, 0], line_sems.at[k, 1], peer)

    def end_plane(k):
        many(plane_buf.at[k], 15, plane_sems.at[k], 1)
        return jnp.sum(plane_buf[k], axis=0)

    def end_line(k):
        many(line_buf.at[k], 15, line_sems.at[k], 1)
        return jnp.sum(line_buf[k], axis=0)

    def scalars(m, n):
        return [jnp.zeros((1, 128), F32)] * 6 + [jnp.broadcast_to(m, (1, 128)), jnp.broadcast_to(n, (1, 128))]

    lines_p, part_l = products(r0p, r0l)
    start_plane(0, packed(lines_p))
    start_line(0, part_l)
    mine = pl.ds(pl.multiple_of(z * 128, 128), 128)
    for b in range(6):
        place = pl.ds((b % 3) * 128, 128)
        x_t[:, b * 128 : (b + 1) * 128] = xl[b // 3, place, mine].astype(F32).T
        h_t[:, b * 128 : (b + 1) * 128] = hl[b // 3, place, mine].astype(F32).T
    w0p = end_plane(0) + DAMP * r0p
    w0l = end_line(0) + DAMP * r0l
    m0, m1 = total_of(r0l * r0l), total_of(r0l * w0l)
    lines_p, part_l = products(w0p, w0l)
    start_plane(1, packed(lines_p + scalars(m0, m1)[6:]))
    start_line(1, part_l)
    got = end_plane(1)
    u0p = got + DAMP * w0p
    u0l = end_line(1) + DAMP * w0l
    rr0, rw0 = got[6:7, :], got[7:8, :]
    al0 = rr0 / rw0
    r1l, w1l = r0l - al0 * w0l, w0l - al0 * u0l
    w1p = w0p - al0 * u0p
    m0, m1 = total_of(r1l * r1l), total_of(r1l * w1l)
    start_plane(2, packed(scalars(m0, m1)))
    _, part_l = products(w1p, None)
    start_line(2, part_l)
    got = end_plane(2)
    u1l = end_line(2) + DAMP * w1l
    rr1, rw1 = got[6:7, :], got[7:8, :]
    be0 = rr1 / rr0
    al1 = rr1 / (rw1 - be0 * rr1 / al0)
    d1 = r1l + be0 * r0l
    r2l = r1l - al1 * (w1l + be0 * w0l)
    w2l = w1l - al1 * (u1l + be0 * u0l)
    m0, m1 = total_of(r2l * r2l), total_of(r2l * w2l)
    start_plane(3, packed(scalars(m0, m1)))
    got = end_plane(3)
    rr2, rw2 = got[6:7, :], got[7:8, :]
    be1 = rr2 / rr1
    al2 = rr2 / (rw2 - be1 * rr2 / al1)
    sol = al0 * r0l + al1 * d1 + al2 * (r2l + be1 * d1)

    across = jnp.concatenate([sol[b : b + 1, :] for b in range(6)], axis=1)

    def summed(turned_ref, right):
        left = jnp.concatenate(
            [turned_ref[pl.ds(pl.multiple_of(c * 32 + 64 * k, 32), 32), :] for k in range(2)], axis=0
        )
        left = left * across
        coarse = left.astype(BF16)
        fine = (left - coarse.astype(F32)).astype(BF16)
        both = dot(jnp.concatenate([coarse, fine], axis=0), right[...].reshape(SET, 1024))
        return -LEARN * (both[0:64] + both[64:128])

    one = summed(x_t, il)
    two = summed(h_t, ol)
    sub_wide = lax.broadcasted_iota(jnp.int32, (8, 1024), 0)
    for e in range(8):
        f, s = one[8 * e : 8 * e + 8], two[8 * e : 8 * e + 8]
        out_send[2 * e] = jnp.where(sub_wide < 4, f, pltpu.roll(s, 4, 0)).astype(BF16)
        out_send[2 * e + 1] = jnp.where(sub_wide < 4, pltpu.roll(f, 4, 0), s).astype(BF16)
    for k in range(1, 16):
        dest = lax.rem(y + k // 4, 4) * 4 + lax.rem(x + k % 4, 4)
        send(out_send.at[dest], out_recv.at[me_p], out_sems.at[0], out_sems.at[1], plane_peers[k - 1])
    out_recv[me_p] = out_send[me_p]
    many(out_recv, 15, out_sems, 1)
    result = jnp.sum(out_recv[...].astype(F32), axis=0)
    out_ref[:, 0:1024] = result[0:4]
    out_ref[:, 1024:2048] = result[4:8]

    for copy in pending + core_copies:
        copy.wait_send()
    many(side_p, 15, sp_sems, 0)
    many(side_l, 7, sl_sems, 0)
    for k in range(4):
        many(plane_buf.at[k], 15, plane_sems.at[k], 0)
    for k in range(3):
        many(line_buf.at[k], 15, line_sems.at[k], 0)
    many(out_send, 15, out_sems, 0)


def shards(inputs, first_weight, second_weight, readout, target, counts, views):
    angle = (2.0 * jnp.pi / VIEWS) * views.astype(F32)
    weight_rows = counts.astype(F32) / 16.0 * (1.0 + 0.5 * jnp.cos(angle))
    side = jnp.pad(jnp.stack([weight_rows, target]), ((0, 6), (0, 128 - CHUNK)))
    vmem = pl.BlockSpec(memory_space=pltpu.VMEM)
    hbm = pl.BlockSpec(memory_space=pltpu.HBM)
    dma = pltpu.SemaphoreType.DMA
    return pl.pallas_call(
        step_kernel,
        out_shape=jax.ShapeDtypeStruct((4, 2048), F32),
        in_specs=[hbm, hbm, hbm, vmem, vmem],
        out_specs=vmem,
        scratch_shapes=[
            pltpu.VMEM((1024, 1024), BF16), pltpu.VMEM((1024, 1024), BF16),
            pltpu.VMEM((SET, 512), BF16), pltpu.VMEM((SET, 512), BF16),
            pltpu.VMEM((SET, 1024), BF16), pltpu.VMEM((SET, 1024), BF16), pltpu.VMEM((SET, 1024), BF16),
            pltpu.VMEM((2, HALF, 1024), BF16), pltpu.VMEM((2, HALF, 1024), BF16),
            pltpu.VMEM((2, HALF, 1024), BF16), pltpu.VMEM((2, HALF, 1024), BF16),
            pltpu.VMEM((HALF, 1024), F32), pltpu.VMEM((2, HALF, SET), F32),
            pltpu.VMEM((16, 8, 128), F32), pltpu.VMEM((8, 8, 128), F32), pltpu.VMEM((128, 128), F32),
            pltpu.VMEM((SET, 128), F32), pltpu.VMEM((SET, 128), F32),
            pltpu.VMEM((HALF, 128), F32), pltpu.VMEM((HALF, 128), F32), pltpu.VMEM((HALF, 128), F32),
            pltpu.VMEM((2, 8, 128), F32), pltpu.VMEM((128, SET), F32), pltpu.VMEM((128, SET), F32),
            pltpu.VMEM((4, 16, 8, 128), F32), pltpu.VMEM((3, 16, 8, 128), F32),
            pltpu.VMEM((16, 8, 1024), BF16), pltpu.VMEM((16, 8, 1024), BF16),
            dma((5,)), dma((8,)), dma((8,)), dma((16,)), dma((16,)), dma((8,)), dma((8,)),
            dma((5,)), dma((5,)), dma((2,)), dma((2,)), dma((4, 2)), dma((3, 2)), dma((2,)),
        ],
        compiler_params=pltpu.CompilerParams(
            collective_id=0, has_side_effects=True, vmem_limit_bytes=56 * 1024 * 1024
        ),
    )(inputs, first_weight, second_weight, side, readout.astype(F32).reshape(1, 1024))


def solution(mesh):
    split = Mesh(mesh.devices.reshape(8, 2, 2, 2, 4), AXES)
    return jax.shard_map(
        shards,
        mesh=split,
        in_specs=(P(AXES, None), P(), P(), P(), P(AXES), P(AXES), P(AXES)),
        out_specs=P(AXES, None),
        check_vma=False,
    )
```

time: 466 us -> 82.1 us (0.18)
  blocking collectives: 225 us -> 0 us
  waiting for transfers between devices: 142 us -> 0 us
  Pallas kernels: 0 us -> 77.3 us
  matrix products: 54.9 us -> 0 us
  between operations: 23.1 us -> 0.01 us
  starting transfers between devices: 6.69 us -> 0 us
    all_gather x2 -> x0, waiting for transfers between devices: 134 us -> none  [in_one_piece(): lax.all_gather(both, axis, axis=dim, tiled=True)]
    psum x15 -> x0, blocking collectives: 118 us -> none  [by_axis(): return functools.reduce(lax.psum, axes, shard)]
    all_to_all x7 -> x0, blocking collectives: 107 us -> none  [the longest x3 57.7 us: from_everyone(): return lax.all_to_all(copies, axis, split_axis=0, concat_axis=0, tiled=True)]
    pallas_call x0 -> x1, Pallas kernels: none -> 77.3 us  [shards(): pl.pallas_call(step_kernel, out_shape=jax.ShapeDtypeStruct((4, 2048), F32...]
    dot_general x13 -> x0, matrix products: 54.9 us -> none  [the longest x4 24.9 us: gram(): lax.dot_general(left, other, (((1,), (1,)), ((), ())), preferred_element_...]
    all_to_all x2 -> x0, waiting for transfers between devices: 7.4 us -> none  [the longest x1 4.88 us: summed_on_arrival(): lax.all_to_all(in_blocks(shard, dim, devices), axis, 0, 0, tiled=True)]
    all_to_all x2 -> x0, starting transfers between devices: 6.62 us -> none  [the longest x1 3.31 us: summed_on_arrival(): lax.all_to_all(in_blocks(shard, dim, devices), axis, 0, 0, tiled=True)]
  transfers between devices with their start and end apart: 4 -> 0, of which waited for: 4 -> 0; matrix products, arithmetic and copies ran while one was open for 1% -> 0% of each run, Pallas kernels for 0% -> 0%
where the time goes in v1:
time: 82.1 us; the launch traced here: 81.9 us
  Pallas kernels  77.3 us (94%)
  other arithmetic  3.24 us (4%)
  local copies, waits for them, and re-layouts  1.38 us (2%)
    pallas_call x1, Pallas kernels, shards(): pl.pallas_call(step_kernel, out_shape=jax.ShapeDtypeStruct((4, 2048), F32...  77.3 us
    another operation x2, other arithmetic, shards(): side = jnp.pad(jnp.stack([weight_rows, target]), ((0, 6), (0, 128 - CHUNK)))  1.98 us

profile of v1, /device:TPU:1, one launch (start us, length us, event | category | flops | bytes accessed | tf_op | source)
XLA Modules:
  0.0 81.9 jit_solution(1269774486717651666)
XLA Ops:
  0.0 0.7 multiply_bitcast_fusion
  0.7 1.3 %select_maximum_fusion.side_ref = f32[8,128]{1,0:T(8,128)} fusion(f32[1,48]{1,0:T(1,128)} %bitcast.5, f32[1,48]{1,0:T(1,128)S(1)} %multiply_bitcast_fusion), kind=kLoop, calls=%fused_computation | loop fusion | flops 8192 | bytes 4480 | tf_op jit(solution)/shard_map/stack | solution.py:406
  2.0 1.3 %reshape.7 = f32[1024]{0:T(1024)} convert(bf16[1024]{0:T(1024)(128)(2,1)} %param.10) | non-fusion elementwise | flops 1024 | bytes 6144 | tf_op jit(solution)/shard_map/reshape | solution.py:434
  3.2 77.3 %shard_map.73 = f32[4,2048]{1,0:T(4,128)} custom-call(bf16[48,1024]{1,0:T(8,128)(2,1)} %x_hbm.1, bf16[1024,1024]{1,0:T(8,128)(2,1)} %w1_hbm.1, bf16[1024,1024]{1,0:T(8,128)(2,1)} %w2_hbm.1, f32[8,128]{1,0:T(8,128)} %select_maximum_fusion.side_ref, f32[1,1024]{1,0:T(1,128)} %bitcast.4), custom_call_target="tpu_custom_call" | custom-call | tf_op jit(solution)/shard_map/pallas_call | solution.py:410
  80.5 1.4 %copy.9 = f32[4,2048]{1,0:T(4,128)} copy(f32[4,2048]{1,0:T(4,128)} %shard_map.73) | data formatting | bytes 65536

commit v2 on v1

--- a/solution.py
+++ b/solution.py
@@ -19,6 +19,7 @@
 HALF = 384
 SET = 768
 WIDE = 256
+UNROLL = 4
 NT = (((1,), (1,)), ((), ()))
 
 
@@ -43,8 +44,9 @@
 
 
 def step_kernel(
-    x_hbm, w1_hbm, w2_hbm, side_ref, readout_ref, out_ref,
-    w1, w2, xpa, xpb, hp, op, ip, xl, hl, ol, il, slope1, kern,
+    x_hbm, w1_hbm, w2_hbm, gain_hbm, target_hbm, counts_hbm, views_hbm, out_ref,
+    gain_in, target_in, counts_in, views_in, gain_row, side_ref,
+    w1, w2, xpa, xpb, hp, op, ip, xl, hl, ol, il, slope_p, slope_l, kern,
     side_p, side_l, side_rows, wcol_p, tcol_p, wcol_l, tcol_l, sig,
     half_r, x_t, h_t, plane_buf, line_buf, out_send, out_recv,
     load_sem, a_send, a_recv, b_send, b_recv, z_send, z_recv,
@@ -81,8 +83,12 @@
         pltpu.make_async_copy(x_hbm.at[:, pl.ds(0, 512)], xpa.at[rows(me_p)], load_sem.at[0]),
         pltpu.make_async_copy(x_hbm.at[:, pl.ds(512, 512)], xpb.at[rows(me_p)], load_sem.at[1]),
         pltpu.make_async_copy(x_hbm, xl.at[c, rows(z)], load_sem.at[2]),
-        pltpu.make_async_copy(w1_hbm, w1, load_sem.at[3]),
-        pltpu.make_async_copy(w2_hbm, w2, load_sem.at[4]),
+        pltpu.make_async_copy(counts_hbm, counts_in, load_sem.at[3]),
+        pltpu.make_async_copy(views_hbm, views_in, load_sem.at[4]),
+        pltpu.make_async_copy(target_hbm, target_in, load_sem.at[5]),
+        pltpu.make_async_copy(gain_hbm, gain_in, load_sem.at[6]),
+        pltpu.make_async_copy(w1_hbm, w1, load_sem.at[7]),
+        pltpu.make_async_copy(w2_hbm, w2, load_sem.at[8]),
     ]
     for load in loads:
         load.start()
@@ -90,81 +96,121 @@
     barrier = pltpu.get_barrier_semaphore()
     for peer in plane_peers + line_peers:
         pl.semaphore_signal(barrier, inc=1, device_id=peer, device_id_type=MESH)
+    for load in loads[:7]:
+        load.wait()
+    side_ref[...] = jnp.zeros_like(side_ref)
+    angle = (2.0 * jnp.pi / VIEWS) * views_in[...].astype(F32)
+    side_ref[0:1, 0:CHUNK] = counts_in[...].astype(F32) / 16.0 * (1.0 + 0.5 * jnp.cos(angle))
+    side_ref[1:2, 0:CHUNK] = target_in[...]
+    gain = gain_in[...].astype(F32)
+    for k in range(8):
+        gain_row[:, k * 128 : (k + 1) * 128] = gain[k : k + 1, :]
     pl.semaphore_wait(barrier, 30)
-    for load in loads[:3]:
-        load.wait()
 
     xn, xq = at(xx=x + 1), at(xx=x + 3)
     yn, yq = at(yy=y + 1), at(yy=y + 3)
     zn, zq = at(zz=z + 1), at(zz=z + 7)
-    xm1, xp1 = lax.rem(x + 3, 4), lax.rem(x + 1, 4)
-    ym1, yp1 = lax.rem(y + 3, 4), lax.rem(y + 1, 4)
     pending = []
-
-    def pa(yy, xx):
-        return rows(yy * 4 + xx)
 
     def go(ref, index, ssem, rsem, k, dev):
         copy = send(ref.at[index], ref.at[index], ssem.at[k], rsem.at[k], dev)
         pending.append(copy)
         return copy
 
-    own = rows(me_p)
-    a1 = [go(xpa, (own,), a_send, a_recv, 0, xn), go(xpa, (own,), a_send, a_recv, 1, xq)]
-    b1 = [go(xpb, (own,), b_send, b_recv, 0, yn), go(xpb, (own,), b_send, b_recv, 1, yq)]
-    z1 = [
-        go(xl, (c, rows(z)), z_send, z_recv, 0, zn),
-        go(xl, (c, rows(z)), z_send, z_recv, 1, zq),
-    ]
+    low, high = pl.ds(0, 256), pl.ds(256, 256)
+    offsets = (0, 3, 1, 2)
+
+    class Spread:
+        def __init__(self, ref, place, near, far, ssem, rsem):
+            self.ref, self.place, self.near, self.far = ref, place, near, far
+            self.sems, self.sent = (ssem, rsem), {}
+
+        def go(self, k, d1, d2, dev, lanes=None):
+            index = (rows(self.place(d1, d2)),) + (() if lanes is None else (lanes,))
+            self.sent[k] = go(self.ref, index, *self.sems, k, dev)
+
+        def arrived(self, *keys):
+            for k in keys:
+                self.sent[k].wait_recv()
+
+        def second(self, j):
+            for side in range(2):
+                self.go(4 + 4 * side + j, offsets[j], 0, self.far[side])
+
+        def step(self, k):
+            if k == 0:
+                self.go(0, 0, 0, self.near[0])
+                self.go(1, 0, 0, self.near[1])
+                self.second(0)
+            elif k == 1:
+                self.arrived(0)
+                self.go(2, 3, 0, self.near[0], low)
+                self.arrived(1)
+                self.go(3, 1, 0, self.near[1], high)
+                self.second(1)
+                self.second(2)
+            elif k == 2:
+                self.arrived(4, 8)
+                self.go(12, 0, 3, self.far[0])
+            elif k == 3:
+                self.arrived(2, 3)
+                self.second(3)
+            elif k == 4:
+                self.arrived(5, 9)
+                self.go(13, 3, 1, self.far[1])
+                self.arrived(6, 10)
+                self.go(14, 1, 1, self.far[1])
+            elif k == 5:
+                self.arrived(7, 11)
+                self.go(15, 2, 3, self.far[0])
+            else:
+                self.arrived(12, 13, 14, 15)
+
+    half_a = Spread(
+        xpa, lambda d1, d2: lax.rem(y + d2, 4) * 4 + lax.rem(x + d1, 4), (xn, xq), (yn, yq), a_send, a_recv
+    )
+    half_b = Spread(
+        xpb, lambda d1, d2: lax.rem(y + d1, 4) * 4 + lax.rem(x + d2, 4), (yn, yq), (xn, xq), b_send, b_recv
+    )
+    ring_sent = {}
+    parts = (pl.ds(0, 512), pl.ds(512, 512))
+
+    def ring(step, side, h):
+        owner = lax.rem(z + (8 - step if side == 0 else step), 8)
+        key = step * 4 + side * 2 + h
+        ring_sent[key] = go(xl, (c, rows(owner), parts[h]), z_send, z_recv, key, (zn, zq)[side])
+
+    def ring_step(step, h):
+        for side in range(2):
+            ring_sent[(step - 1) * 4 + side * 2 + h].wait_recv()
+            if step < 3 or side == h:
+                ring(step, side, h)
+
+    half_a.step(0)
+    half_b.step(0)
+    for h in range(2):
+        for side in range(2):
+            ring(0, side, h)
     for k in range(15):
         send(side_ref, side_p.at[me_p], sp_sems.at[0], sp_sems.at[1], plane_peers[k])
     for k in range(7):
         send(side_ref, side_l.at[z], sl_sems.at[0], sl_sems.at[1], line_same[k])
     side_p[me_p] = side_ref[...]
     side_l[z] = side_ref[...]
-
-    low, high = pl.ds(0, 256), pl.ds(256, 256)
-    a1[0].wait_recv()
-    a2 = [go(xpa, (pa(y, xm1), low), a_send, a_recv, 2, xn)]
-    a1[1].wait_recv()
-    a2 += [go(xpa, (pa(y, xp1), high), a_send, a_recv, 3, xq)]
-    b1[0].wait_recv()
-    b2 = [go(xpb, (pa(ym1, x), low), b_send, b_recv, 2, yn)]
-    b1[1].wait_recv()
-    b2 += [go(xpb, (pa(yp1, x), high), b_send, b_recv, 3, yq)]
-
-    def ring(step, before):
-        down, up = lax.rem(z + 8 - step, 8), lax.rem(z + step, 8)
-        lanes = (slice(None), slice(None)) if step < 3 else (pl.ds(0, 512), pl.ds(512, 512))
-        before[0].wait_recv()
-        one = go(xl, (c, rows(down), lanes[0]), z_send, z_recv, 2 * step, zn)
-        before[1].wait_recv()
-        two = go(xl, (c, rows(up), lanes[1]), z_send, z_recv, 2 * step + 1, zq)
-        return [one, two]
-
-    z2 = ring(1, z1)
-    for copy in a2:
-        copy.wait_recv()
-    line_y = (rows(y * 4, 4),)
-    a3 = [go(xpa, line_y, a_send, a_recv, 4, yn), go(xpa, line_y, a_send, a_recv, 5, yq)]
-    for copy in b2:
-        copy.wait_recv()
-    b3 = []
-    for side, dev in ((0, xn), (1, xq)):
-        b3.append([go(xpb, (pa(yy, x),), b_send, b_recv, 4 + 4 * side + yy, dev) for yy in range(4)])
-    z3 = ring(2, z2)
-    a3[0].wait_recv()
-    a4 = [go(xpa, (rows(ym1 * 4, 2),), a_send, a_recv, 6, yn)]
-    a3[1].wait_recv()
-    a4 += [go(xpa, (rows(yp1 * 4 + 2, 2),), a_send, a_recv, 7, yq)]
-    b4 = []
-    for copy in b3[0]:
-        copy.wait_recv()
-    b4 += [go(xpb, (pa(yy, xm1),), b_send, b_recv, 12 + yy, xn) for yy in range(2)]
-    for copy in b3[1]:
-        copy.wait_recv()
-    b4 += [go(xpb, (pa(yy, xp1),), b_send, b_recv, 12 + yy, xq) for yy in range(2, 4)]
-    z4 = ring(3, z3)
+    half_a.step(1)
+    half_b.step(1)
+    ring_step(1, 0)
+    ring_step(1, 1)
+    for k in (2, 3):
+        half_a.step(k)
+        half_b.step(k)
+    ring_step(2, 0)
+    ring_step(2, 1)
+    for k in (4, 5):
+        half_a.step(k)
+        half_b.step(k)
+    ring_step(3, 0)
+    ring_step(3, 1)
 
     def many(ref, count, sems, which):
         view = ref.at[pl.ds(0, count)]
@@ -186,43 +232,35 @@
         place = pl.ds(s * CHUNK, CHUNK)
         wcol_l[place, :] = jnp.broadcast_to(turned[0:CHUNK, 32 + s : 33 + s], (CHUNK, 128))
         tcol_l[place, :] = jnp.broadcast_to(turned[0:CHUNK, 40 + s : 41 + s], (CHUNK, 128))
-    loads[3].wait()
-    loads[4].wait()
+    loads[7].wait()
+    loads[8].wait()
 
     def wide(n):
         return pl.ds(pl.multiple_of(n * WIDE, WIDE), WIDE)
 
-    def forward(x_parts, h_ref, o_ref, i_ref, wcol, tcol, after):
-        def first(n, carry):
+    def first(x_parts, h_ref, slope_ref):
+        def body(n, carry):
             pre = sum(dot(part[...], w1[lo : lo + size, wide(n)]) for part, lo, size in x_parts)
             s = sigmoid(pre)
             h_ref[:, wide(n)] = (pre * s).astype(BF16)
-            slope1[:, wide(n)] = s * (1.0 + pre * (1.0 - s))
+            slope_ref[:, wide(n)] = s * (1.0 + pre * (1.0 - s))
             return carry
 
-        lax.fori_loop(0, 4, first, 0)
-        after(0)
+        lax.fori_loop(0, 4, body, 0, unroll=UNROLL)
+
+    def second(h_ref, o_ref, wcol, tcol):
         sig[...] = jnp.zeros_like(sig)
 
-        def second(n, carry):
+        def body(n, carry):
             pre = dot(h_ref[...], w2[:, wide(n)])
             s = sigmoid(pre)
-            gain = readout_ref[0:1, wide(n)]
-            parts = pre * s * gain
-            sig[...] += parts[:, 0:128] + parts[:, 128:256]
+            gain = gain_row[0:1, wide(n)]
+            silu = pre * s * gain
+            sig[...] += silu[:, 0:128] + silu[:, 128:256]
             o_ref[:, wide(n)] = (twice(wcol[...]) * (s * (1.0 + pre * (1.0 - s))) * gain).astype(BF16)
             return carry
 
-        lax.fori_loop(0, 4, second, 0)
-        after(1)
-
-        def third(n, carry):
-            back = dot_nt(o_ref[...], w2[wide(n), :])
-            i_ref[:, wide(n)] = (back * slope1[:, wide(n)]).astype(BF16)
-            return carry
-
-        lax.fori_loop(0, 4, third, 0)
-        after(2)
+        lax.fori_loop(0, 4, body, 0, unroll=UNROLL)
         lane = lax.broadcasted_iota(jnp.int32, (128, 128), 1)
         found = []
         for b in range(3):
@@ -231,6 +269,14 @@
             found.append(jnp.sum(term.T, axis=0, keepdims=True))
         return found
 
+    def third(o_ref, i_ref, slope_ref):
+        def body(n, carry):
+            back = dot_nt(o_ref[...], w2[wide(n), :])
+            i_ref[:, wide(n)] = (back * slope_ref[:, wide(n)]).astype(BF16)
+            return carry
+
+        lax.fori_loop(0, 4, body, 0, unroll=UNROLL)
+
     sub = lax.broadcasted_iota(jnp.int32, (8, 128), 0)
 
     def packed(lines, first=0):
@@ -239,29 +285,31 @@
             value = jnp.where(sub == first + k, line, value)
         return value
 
-    for copy in z4:
-        copy.wait_recv()
+    for key in (12, 15):
+        ring_sent[key].wait_recv()
     partner = at(cc=1 - c)
-    core_copies = [send(xl.at[c], xl.at[c], core_send.at[0], core_recv.at[0], partner)]
-
-    def share(k):
-        ref = (hl, ol, il)[k]
-        core_copies.append(send(ref.at[c], ref.at[c], core_send.at[1 + k], core_recv.at[1 + k], partner))
-
-    found = forward([(xl.at[c], 0, 1024)], hl.at[c], ol.at[c], il.at[c], wcol_l, tcol_l, share)
-    half_r[c] = packed(found, c * 3)
-    core_copies.append(send(half_r.at[c], half_r.at[c], core_send.at[4], core_recv.at[4], partner))
-
-    for copy in a4 + b4:
-        copy.wait_recv()
+    core_copies = []
+
+    def share(k, ref):
+        core_copies.append(send(ref.at[c], ref.at[c], core_send.at[k], core_recv.at[k], partner))
+
+    share(0, xl)
+    first([(xl.at[c], 0, 1024)], hl.at[c], slope_l)
+    share(1, hl)
+    half_a.step(6)
+    half_b.step(6)
+    blocks = [pl.ds(b * HALF, HALF) for b in range(2)]
+    for b in blocks:
+        first([(xpa.at[b], 0, 512), (xpb.at[b], 512, 512)], hp.at[b], slope_p.at[b])
+    half_r[c] = packed(second(hl.at[c], ol.at[c], wcol_l, tcol_l), c * 3)
+    share(2, ol)
+    share(4, half_r)
+    third(ol.at[c], il.at[c], slope_l)
+    share(3, il)
     found = []
-    for b in range(2):
-        place = pl.ds(b * HALF, HALF)
-        found += forward(
-            [(xpa.at[place], 0, 512), (xpb.at[place], 512, 512)],
-            hp.at[place], op.at[place], ip.at[place], wcol_p.at[place], tcol_p.at[place],
-            lambda k: None,
-        )
+    for b in blocks:
+        found += second(hp.at[b], op.at[b], wcol_p.at[b], tcol_p.at[b])
+        third(op.at[b], ip.at[b], slope_p.at[b])
     r0p = packed(found)
 
     def gram(which):
@@ -273,7 +321,7 @@
             kern[which, :, place] = value
             return carry
 
-        lax.fori_loop(0, 3, block, 0)
+        lax.fori_loop(0, 3, block, 0, unroll=3)
 
     gram(c)
     for copy in core_copies:
@@ -401,37 +449,40 @@
 
 
 def shards(inputs, first_weight, second_weight, readout, target, counts, views):
-    angle = (2.0 * jnp.pi / VIEWS) * views.astype(F32)
-    weight_rows = counts.astype(F32) / 16.0 * (1.0 + 0.5 * jnp.cos(angle))
-    side = jnp.pad(jnp.stack([weight_rows, target]), ((0, 6), (0, 128 - CHUNK)))
     vmem = pl.BlockSpec(memory_space=pltpu.VMEM)
     hbm = pl.BlockSpec(memory_space=pltpu.HBM)
     dma = pltpu.SemaphoreType.DMA
     return pl.pallas_call(
         step_kernel,
         out_shape=jax.ShapeDtypeStruct((4, 2048), F32),
-        in_specs=[hbm, hbm, hbm, vmem, vmem],
+        in_specs=[hbm] * 7,
         out_specs=vmem,
         scratch_shapes=[
+            pltpu.VMEM((8, 128), BF16), pltpu.VMEM((1, CHUNK), F32),
+            pltpu.VMEM((1, CHUNK), jnp.int32), pltpu.VMEM((1, CHUNK), jnp.int32),
+            pltpu.VMEM((1, 1024), F32), pltpu.VMEM((8, 128), F32),
             pltpu.VMEM((1024, 1024), BF16), pltpu.VMEM((1024, 1024), BF16),
             pltpu.VMEM((SET, 512), BF16), pltpu.VMEM((SET, 512), BF16),
             pltpu.VMEM((SET, 1024), BF16), pltpu.VMEM((SET, 1024), BF16), pltpu.VMEM((SET, 1024), BF16),
             pltpu.VMEM((2, HALF, 1024), BF16), pltpu.VMEM((2, HALF, 1024), BF16),
             pltpu.VMEM((2, HALF, 1024), BF16), pltpu.VMEM((2, HALF, 1024), BF16),
-            pltpu.VMEM((HALF, 1024), F32), pltpu.VMEM((2, HALF, SET), F32),
+            pltpu.VMEM((SET, 1024), F32), pltpu.VMEM((HALF, 1024), F32), pltpu.VMEM((2, HALF, SET), F32),
             pltpu.VMEM((16, 8, 128), F32), pltpu.VMEM((8, 8, 128), F32), pltpu.VMEM((128, 128), F32),
             pltpu.VMEM((SET, 128), F32), pltpu.VMEM((SET, 128), F32),
             pltpu.VMEM((HALF, 128), F32), pltpu.VMEM((HALF, 128), F32), pltpu.VMEM((HALF, 128), F32),
             pltpu.VMEM((2, 8, 128), F32), pltpu.VMEM((128, SET), F32), pltpu.VMEM((128, SET), F32),
             pltpu.VMEM((4, 16, 8, 128), F32), pltpu.VMEM((3, 16, 8, 128), F32),
             pltpu.VMEM((16, 8, 1024), BF16), pltpu.VMEM((16, 8, 1024), BF16),
-            dma((5,)), dma((8,)), dma((8,)), dma((16,)), dma((16,)), dma((8,)), dma((8,)),
+            dma((9,)), dma((16,)), dma((16,)), dma((16,)), dma((16,)), dma((16,)), dma((16,)),
             dma((5,)), dma((5,)), dma((2,)), dma((2,)), dma((4, 2)), dma((3, 2)), dma((2,)),
         ],
         compiler_params=pltpu.CompilerParams(
             collective_id=0, has_side_effects=True, vmem_limit_bytes=56 * 1024 * 1024
         ),
-    )(inputs, first_weight, second_weight, side, readout.astype(F32).reshape(1, 1024))
+    )(
+        inputs, first_weight, second_weight, readout.reshape(8, 128),
+        target.reshape(1, CHUNK), counts.reshape(1, CHUNK), views.reshape(1, CHUNK),
+    )
 
 
 def solution(mesh):

time: 82.1 us -> 72 us (0.88)
  Pallas kernels: 77.3 us -> 70.2 us
  other arithmetic: 3.24 us -> 0 us
    pallas_call x1, Pallas kernels: 77.3 us -> 70.2 us  [shards(): pl.pallas_call(step_kernel, out_shape=jax.ShapeDtypeStruct((4, 2048), F32...]
    another operation x2 -> x0, other arithmetic: 1.98 us -> none  [shards(): side = jnp.pad(jnp.stack([weight_rows, target]), ((0, 6), (0, 128 - CHUNK)))]
    reshape x1 -> x0, other arithmetic: 1.27 us -> none  [shards(): readout.astype(F32).reshape(1, 1024)]
where the time goes in v2:
time: 72 us; the launch traced here: 71.6 us
  Pallas kernels  70.2 us (98%)
  local copies, waits for them, and re-layouts  1.38 us (2%)
    pallas_call x1, Pallas kernels, shards(): pl.pallas_call(step_kernel, out_shape=jax.ShapeDtypeStruct((4, 2048), F32...  70.2 us

profile of v2, /device:TPU:1, one launch (start us, length us, event | category | flops | bytes accessed | tf_op | source)
XLA Modules:
  0.0 71.6 jit_solution(5034489037148545836)
XLA Ops:
  0.0 70.2 %shard_map.73 = f32[4,2048]{1,0:T(4,128)} custom-call(bf16[48,1024]{1,0:T(8,128)(2,1)} %x_hbm.1, bf16[1024,1024]{1,0:T(8,128)(2,1)} %w1_hbm.1, bf16[1024,1024]{1,0:T(8,128)(2,1)} %w2_hbm.1, bf16[8,128]{1,0:T(8,128)(2,1)} %bitcast.4, f32[1,48]{1,0:T(1,128)} %bitcast.5, s32[1,48]{1,0:T(1,128)} %bitcast.6, s32[1,48]{1,0:T(1,128)} %bitcast.7), custom_call_target="tpu_custom_call" | custom-call | tf_op jit(solution)/shard_map/pallas_call | solution.py:455
  70.2 1.4 %copy.9 = f32[4,2048]{1,0:T(4,128)} copy(f32[4,2048]{1,0:T(4,128)} %shard_map.73) | data formatting | bytes 65536

commit v3 on v2

--- a/solution.py
+++ b/solution.py
@@ -19,7 +19,6 @@
 HALF = 384
 SET = 768
 WIDE = 256
-UNROLL = 4
 NT = (((1,), (1,)), ((), ()))
 
 
@@ -46,8 +45,8 @@
 def step_kernel(
     x_hbm, w1_hbm, w2_hbm, gain_hbm, target_hbm, counts_hbm, views_hbm, out_ref,
     gain_in, target_in, counts_in, views_in, gain_row, side_ref,
-    w1, w2, xpa, xpb, hp, op, ip, xl, hl, ol, il, slope_p, slope_l, kern,
-    side_p, side_l, side_rows, wcol_p, tcol_p, wcol_l, tcol_l, sig,
+    w1, w2, xpa, xpb, hp, op, ip, xl, hl, ol, il, xs, hs, os, slope, wcol, kern,
+    side_p, side_l, side_rows, wcol_p, tcol_p, wcol_l, tcol_l, sig, q_p, q_l,
     half_r, x_t, h_t, plane_buf, line_buf, out_send, out_recv,
     load_sem, a_send, a_recv, b_send, b_recv, z_send, z_recv,
     core_send, core_recv, sp_sems, sl_sems, plane_sems, line_sems, out_sems,
@@ -137,34 +136,35 @@
             for side in range(2):
                 self.go(4 + 4 * side + j, offsets[j], 0, self.far[side])
 
-        def step(self, k):
-            if k == 0:
-                self.go(0, 0, 0, self.near[0])
-                self.go(1, 0, 0, self.near[1])
-                self.second(0)
-            elif k == 1:
+        def start(self):
+            self.go(0, 0, 0, self.near[0])
+            self.go(1, 0, 0, self.near[1])
+            self.second(0)
+
+        def hop(self, k):
+            if k == 1:
                 self.arrived(0)
                 self.go(2, 3, 0, self.near[0], low)
                 self.arrived(1)
                 self.go(3, 1, 0, self.near[1], high)
                 self.second(1)
                 self.second(2)
-            elif k == 2:
                 self.arrived(4, 8)
                 self.go(12, 0, 3, self.far[0])
-            elif k == 3:
+            elif k == 2:
                 self.arrived(2, 3)
                 self.second(3)
-            elif k == 4:
                 self.arrived(5, 9)
                 self.go(13, 3, 1, self.far[1])
                 self.arrived(6, 10)
                 self.go(14, 1, 1, self.far[1])
-            elif k == 5:
+                self.arrived(12)
+            elif k == 3:
                 self.arrived(7, 11)
                 self.go(15, 2, 3, self.far[0])
+                self.arrived(13, 14)
             else:
-                self.arrived(12, 13, 14, 15)
+                self.arrived(15)
 
     half_a = Spread(
         xpa, lambda d1, d2: lax.rem(y + d2, 4) * 4 + lax.rem(x + d1, 4), (xn, xq), (yn, yq), a_send, a_recv
@@ -186,96 +186,121 @@
             if step < 3 or side == h:
                 ring(step, side, h)
 
-    half_a.step(0)
-    half_b.step(0)
-    for h in range(2):
-        for side in range(2):
-            ring(0, side, h)
     for k in range(15):
         send(side_ref, side_p.at[me_p], sp_sems.at[0], sp_sems.at[1], plane_peers[k])
     for k in range(7):
         send(side_ref, side_l.at[z], sl_sems.at[0], sl_sems.at[1], line_same[k])
+    half_a.start()
+    half_b.start()
+    for h in range(2):
+        for side in range(2):
+            ring(0, side, h)
     side_p[me_p] = side_ref[...]
     side_l[z] = side_ref[...]
-    half_a.step(1)
-    half_b.step(1)
-    ring_step(1, 0)
-    ring_step(1, 1)
-    for k in (2, 3):
-        half_a.step(k)
-        half_b.step(k)
-    ring_step(2, 0)
-    ring_step(2, 1)
-    for k in (4, 5):
-        half_a.step(k)
-        half_b.step(k)
-    ring_step(3, 0)
-    ring_step(3, 1)
+
+    def hop(k):
+        half_a.hop(k)
+        half_b.hop(k)
+        if k < 4:
+            ring_step(k, 0)
+            ring_step(k, 1)
+        else:
+            for key in (12, 15):
+                ring_sent[key].wait_recv()
+
+    near = {0: ((0, 0),), 1: ((0, 1), (0, 3), (1, 0), (3, 0)),
+            2: ((2, 0), (0, 2), (1, 1), (1, 3), (3, 1), (3, 3)),
+            3: ((2, 1), (2, 3), (1, 2), (3, 2)), 4: ((2, 2),)}
+
+    def plane_slots(k):
+        return [lax.rem(y + dy, 4) * 4 + lax.rem(x + dx, 4) for dx, dy in near[k]]
+
+    def line_slots(k):
+        return [lax.rem(z + d, 8) for d in ((k,) if k in (0, 4) else (k, 8 - k))]
 
     def many(ref, count, sems, which):
         view = ref.at[pl.ds(0, count)]
         pltpu.make_async_copy(view, view, sems.at[which]).wait()
 
-    many(side_p, 15, sp_sems, 1)
-    many(side_l, 7, sl_sems, 1)
-    side_rows[...] = jnp.zeros_like(side_rows)
-    side_rows[0:16, :] = side_p[:, 0, :]
-    side_rows[16:32, :] = side_p[:, 1, :]
-    side_rows[32:40, :] = side_l[:, 0, :]
-    side_rows[40:48, :] = side_l[:, 1, :]
-    turned = side_rows[...].T
-    for s in range(16):
-        place = pl.ds(s * CHUNK, CHUNK)
-        wcol_p[place, :] = jnp.broadcast_to(turned[0:CHUNK, s : s + 1], (CHUNK, 128))
-        tcol_p[place, :] = jnp.broadcast_to(turned[0:CHUNK, 16 + s : 17 + s], (CHUNK, 128))
-    for s in range(8):
-        place = pl.ds(s * CHUNK, CHUNK)
-        wcol_l[place, :] = jnp.broadcast_to(turned[0:CHUNK, 32 + s : 33 + s], (CHUNK, 128))
-        tcol_l[place, :] = jnp.broadcast_to(turned[0:CHUNK, 40 + s : 41 + s], (CHUNK, 128))
-    loads[7].wait()
-    loads[8].wait()
+    def columns():
+        many(side_p, 15, sp_sems, 1)
+        many(side_l, 7, sl_sems, 1)
+        side_rows[...] = jnp.zeros_like(side_rows)
+        side_rows[0:16, :] = side_p[:, 0, :]
+        side_rows[16:32, :] = side_p[:, 1, :]
+        side_rows[32:40, :] = side_l[:, 0, :]
+        side_rows[40:48, :] = side_l[:, 1, :]
+        turned = side_rows[...].T
+        lane = lax.broadcasted_iota(jnp.int32, (CHUNK, 128), 1)
+        for s in range(16):
+            place = pl.ds(s * CHUNK, CHUNK)
+            wcol_p[place, :] = jnp.broadcast_to(turned[0:CHUNK, s : s + 1], (CHUNK, 128))
+            tcol_p[place, :] = jnp.where(lane == 0, turned[0:CHUNK, 16 + s : 17 + s], 0.0)
+        for s in range(8):
+            place = pl.ds(s * CHUNK, CHUNK)
+            wcol_l[place, :] = jnp.broadcast_to(turned[0:CHUNK, 32 + s : 33 + s], (CHUNK, 128))
+            tcol_l[place, :] = jnp.where(lane == 0, turned[0:CHUNK, 40 + s : 41 + s], 0.0)
 
     def wide(n):
         return pl.ds(pl.multiple_of(n * WIDE, WIDE), WIDE)
 
-    def first(x_parts, h_ref, slope_ref):
-        def body(n, carry):
-            pre = sum(dot(part[...], w1[lo : lo + size, wide(n)]) for part, lo, size in x_parts)
+    def batch(line, plane, middle):
+        chunks = [(xl, hl, ol, il, q_l, wcol_l, tcol_l, slot) for slot in line]
+        chunks += [(None, hp, op, ip, q_p, wcol_p, tcol_p, slot) for slot in plane]
+        size = len(chunks) * CHUNK
+        span = pl.ds(0, size)
+        for k, chunk in enumerate(chunks):
+            to, at_slot = pl.ds(k * CHUNK, CHUNK), rows(chunk[-1])
+            if chunk[0] is None:
+                xs[to, 0:512] = xpa[at_slot, :]
+                xs[to, 512:1024] = xpb[at_slot, :]
+            else:
+                xs[to, :] = xl[c, at_slot, :]
+
+        def put(which, lanes, value):
+            for k, chunk in enumerate(chunks):
+                piece = value[k * CHUNK : (k + 1) * CHUNK]
+                if chunk[0] is None:
+                    chunk[which][rows(chunk[-1]), lanes] = piece
+                else:
+                    chunk[which][c, rows(chunk[-1]), lanes] = piece
+
+        for n in range(4):
+            lanes = pl.ds(n * WIDE, WIDE)
+            pre = dot(xs[span, :], w1[:, lanes])
             s = sigmoid(pre)
-            h_ref[:, wide(n)] = (pre * s).astype(BF16)
-            slope_ref[:, wide(n)] = s * (1.0 + pre * (1.0 - s))
-            return carry
-
-        lax.fori_loop(0, 4, body, 0, unroll=UNROLL)
-
-    def second(h_ref, o_ref, wcol, tcol):
-        sig[...] = jnp.zeros_like(sig)
-
-        def body(n, carry):
-            pre = dot(h_ref[...], w2[:, wide(n)])
+            value = (pre * s).astype(BF16)
+            hs[span, lanes] = value
+            put(1, lanes, value)
+            slope[span, lanes] = s * (1.0 + pre * (1.0 - s))
+        middle()
+        for k, chunk in enumerate(chunks):
+            to, at_slot = pl.ds(k * CHUNK, CHUNK), rows(chunk[-1])
+            wcol[to, :] = chunk[5][at_slot, :]
+        for n in range(4):
+            lanes = pl.ds(n * WIDE, WIDE)
+            pre = dot(hs[span, :], w2[:, lanes])
             s = sigmoid(pre)
-            gain = gain_row[0:1, wide(n)]
+            gain = gain_row[0:1, lanes]
             silu = pre * s * gain
-            sig[...] += silu[:, 0:128] + silu[:, 128:256]
-            o_ref[:, wide(n)] = (twice(wcol[...]) * (s * (1.0 + pre * (1.0 - s))) * gain).astype(BF16)
-            return carry
-
-        lax.fori_loop(0, 4, body, 0, unroll=UNROLL)
-        lane = lax.broadcasted_iota(jnp.int32, (128, 128), 1)
-        found = []
-        for b in range(3):
-            place = pl.ds(b * 128, 128)
-            term = sig[place, :] * wcol[place, :] - jnp.where(lane == 0, tcol[place, :], 0.0)
-            found.append(jnp.sum(term.T, axis=0, keepdims=True))
-        return found
-
-    def third(o_ref, i_ref, slope_ref):
-        def body(n, carry):
-            back = dot_nt(o_ref[...], w2[wide(n), :])
-            i_ref[:, wide(n)] = (back * slope_ref[:, wide(n)]).astype(BF16)
-            return carry
-
-        lax.fori_loop(0, 4, body, 0, unroll=UNROLL)
+            silu = silu[:, 0:128] + silu[:, 128:256]
+            if n == 0:
+                sig[span, :] = silu
+            else:
+                sig[span, :] += silu
+            value = (twice(wcol[span, :]) * (s * (1.0 + pre * (1.0 - s))) * gain).astype(BF16)
+            os[span, lanes] = value
+            put(2, lanes, value)
+        for n in range(4):
+            lanes = pl.ds(n * WIDE, WIDE)
+            back = dot_nt(os[span, :], w2[lanes, :])
+            put(3, lanes, (back * slope[span, lanes]).astype(BF16))
+        for k, chunk in enumerate(chunks):
+            to, at_slot = pl.ds(k * CHUNK, CHUNK), rows(chunk[-1])
+            chunk[4][at_slot, :] = sig[to, :] * wcol[to, :] - chunk[6][at_slot, :]
+        for slot in line:
+            for ref in (xl, hl, ol, il):
+                share(ref.at[c, rows(slot)])
 
     sub = lax.broadcasted_iota(jnp.int32, (8, 128), 0)
 
@@ -285,32 +310,27 @@
             value = jnp.where(sub == first + k, line, value)
         return value
 
-    for key in (12, 15):
-        ring_sent[key].wait_recv()
     partner = at(cc=1 - c)
     core_copies = []
 
-    def share(k, ref):
-        core_copies.append(send(ref.at[c], ref.at[c], core_send.at[k], core_recv.at[k], partner))
-
-    share(0, xl)
-    first([(xl.at[c], 0, 1024)], hl.at[c], slope_l)
-    share(1, hl)
-    half_a.step(6)
-    half_b.step(6)
-    blocks = [pl.ds(b * HALF, HALF) for b in range(2)]
-    for b in blocks:
-        first([(xpa.at[b], 0, 512), (xpb.at[b], 512, 512)], hp.at[b], slope_p.at[b])
-    half_r[c] = packed(second(hl.at[c], ol.at[c], wcol_l, tcol_l), c * 3)
-    share(2, ol)
-    share(4, half_r)
-    third(ol.at[c], il.at[c], slope_l)
-    share(3, il)
-    found = []
-    for b in blocks:
-        found += second(hp.at[b], op.at[b], wcol_p.at[b], tcol_p.at[b])
-        third(op.at[b], ip.at[b], slope_p.at[b])
-    r0p = packed(found)
+    def share(view):
+        k = len(core_copies)
+        core_copies.append(send(view, view, core_send.at[k], core_recv.at[k], partner))
+
+    loads[7].wait()
+    hop(1)
+    loads[8].wait()
+    batch(line_slots(0) + line_slots(1), plane_slots(0) + plane_slots(1), columns)
+    for k in (2, 3, 4):
+        hop(k)
+        batch(line_slots(k), plane_slots(k), lambda: None)
+
+    def as_lines(ref, count):
+        return [jnp.sum(ref[pl.ds(b * 128, 128), :].T, axis=0, keepdims=True) for b in range(count)]
+
+    half_r[c] = packed(as_lines(q_l, 3), c * 3)
+    share(half_r.at[c])
+    r0p = packed(as_lines(q_p, 6))
 
     def gram(which):
         def block(n, carry):
@@ -460,21 +480,24 @@
         scratch_shapes=[
             pltpu.VMEM((8, 128), BF16), pltpu.VMEM((1, CHUNK), F32),
             pltpu.VMEM((1, CHUNK), jnp.int32), pltpu.VMEM((1, CHUNK), jnp.int32),
-            pltpu.VMEM((1, 1024), F32), pltpu.VMEM((8, 128), F32),
+            pltpu.VMEM((1, 1024), F32), pltpu.VMEM((2, 128), F32),
             pltpu.VMEM((1024, 1024), BF16), pltpu.VMEM((1024, 1024), BF16),
             pltpu.VMEM((SET, 512), BF16), pltpu.VMEM((SET, 512), BF16),
             pltpu.VMEM((SET, 1024), BF16), pltpu.VMEM((SET, 1024), BF16), pltpu.VMEM((SET, 1024), BF16),
             pltpu.VMEM((2, HALF, 1024), BF16), pltpu.VMEM((2, HALF, 1024), BF16),
             pltpu.VMEM((2, HALF, 1024), BF16), pltpu.VMEM((2, HALF, 1024), BF16),
-            pltpu.VMEM((SET, 1024), F32), pltpu.VMEM((HALF, 1024), F32), pltpu.VMEM((2, HALF, SET), F32),
-            pltpu.VMEM((16, 8, 128), F32), pltpu.VMEM((8, 8, 128), F32), pltpu.VMEM((128, 128), F32),
+            pltpu.VMEM((HALF, 1024), BF16), pltpu.VMEM((HALF, 1024), BF16), pltpu.VMEM((HALF, 1024), BF16),
+            pltpu.VMEM((HALF, 1024), F32), pltpu.VMEM((HALF, 128), F32),
+            pltpu.VMEM((2, HALF, SET), F32),
+            pltpu.VMEM((16, 2, 128), F32), pltpu.VMEM((8, 2, 128), F32), pltpu.VMEM((128, 128), F32),
             pltpu.VMEM((SET, 128), F32), pltpu.VMEM((SET, 128), F32),
             pltpu.VMEM((HALF, 128), F32), pltpu.VMEM((HALF, 128), F32), pltpu.VMEM((HALF, 128), F32),
+            pltpu.VMEM((SET, 128), F32), pltpu.VMEM((HALF, 128), F32),
             pltpu.VMEM((2, 8, 128), F32), pltpu.VMEM((128, SET), F32), pltpu.VMEM((128, SET), F32),
             pltpu.VMEM((4, 16, 8, 128), F32), pltpu.VMEM((3, 16, 8, 128), F32),
             pltpu.VMEM((16, 8, 1024), BF16), pltpu.VMEM((16, 8, 1024), BF16),
             dma((9,)), dma((16,)), dma((16,)), dma((16,)), dma((16,)), dma((16,)), dma((16,)),
-            dma((5,)), dma((5,)), dma((2,)), dma((2,)), dma((4, 2)), dma((3, 2)), dma((2,)),
+            dma((33,)), dma((33,)), dma((2,)), dma((2,)), dma((4, 2)), dma((3, 2)), dma((2,)),
         ],
         compiler_params=pltpu.CompilerParams(
             collective_id=0, has_side_effects=True, vmem_limit_bytes=56 * 1024 * 1024

time: 72 us -> 64.7 us (0.90)
  Pallas kernels: 70.2 us -> 63.2 us
    pallas_call x1, Pallas kernels: 70.2 us -> 63.2 us  [shards(): pl.pallas_call(step_kernel, out_shape=jax.ShapeDtypeStruct((4, 2048), F32...]
where the time goes in v3:
time: 64.7 us; the launch traced here: 64.6 us
  Pallas kernels  63.2 us (98%)
  local copies, waits for them, and re-layouts  1.38 us (2%)
    pallas_call x1, Pallas kernels, shards(): pl.pallas_call(step_kernel, out_shape=jax.ShapeDtypeStruct((4, 2048), F32...  63.2 us
    unnamed x1, local copies, waits for them, and re-layouts  1.38 us

profile of v3, /device:TPU:1, one launch (start us, length us, event | category | flops | bytes accessed | tf_op | source)
XLA Modules:
  0.0 64.6 jit_solution(10293858341358038111)
XLA Ops:
  0.0 63.2 %shard_map.73 = f32[4,2048]{1,0:T(4,128)} custom-call(bf16[48,1024]{1,0:T(8,128)(2,1)} %x_hbm.1, bf16[1024,1024]{1,0:T(8,128)(2,1)} %w1_hbm.1, bf16[1024,1024]{1,0:T(8,128)(2,1)} %w2_hbm.1, bf16[8,128]{1,0:T(8,128)(2,1)} %bitcast.4, f32[1,48]{1,0:T(1,128)} %bitcast.5, s32[1,48]{1,0:T(1,128)} %bitcast.6, s32[1,48]{1,0:T(1,128)} %bitcast.7), custom_call_target="tpu_custom_call" | custom-call | tf_op jit(solution)/shard_map/pallas_call | solution.py:475
  63.2 1.4 %copy.9 = f32[4,2048]{1,0:T(4,128)} copy(f32[4,2048]{1,0:T(4,128)} %shard_map.73) | data formatting | bytes 65536

commit v4 on v3

--- a/solution.py
+++ b/solution.py
@@ -47,7 +47,7 @@
     gain_in, target_in, counts_in, views_in, gain_row, side_ref,
     w1, w2, xpa, xpb, hp, op, ip, xl, hl, ol, il, xs, hs, os, slope, wcol, kern,
     side_p, side_l, side_rows, wcol_p, tcol_p, wcol_l, tcol_l, sig, q_p, q_l,
-    half_r, x_t, h_t, plane_buf, line_buf, out_send, out_recv,
+    half_r, x_t, h_t, terms, plane_buf, line_buf, out_send, out_recv,
     load_sem, a_send, a_recv, b_send, b_recv, z_send, z_recv,
     core_send, core_recv, sp_sems, sl_sems, plane_sems, line_sems, out_sems,
 ):
@@ -63,9 +63,11 @@
         cc = c if cc is None else cc
         return (zz, yy // 2, cc, lax.rem(yy, 2), xx)
 
-    plane_peers = [at(xx=x + k % 4, yy=y + k // 4) for k in range(1, 16)]
-    line_same = [at(zz=z + k) for k in range(1, 8)]
-    line_peers = line_same + [at(zz=z + k, cc=1 - c) for k in range(8)]
+    plane_order = (10, 6, 14, 9, 11, 2, 8, 5, 7, 13, 15, 1, 3, 4, 12)
+    line_order = (4, 3, 5, 2, 6, 1, 7)
+    plane_peers = [at(xx=x + k % 4, yy=y + k // 4) for k in plane_order]
+    line_same = [at(zz=z + k) for k in line_order]
+    line_peers = [at(zz=z + k, cc=c if q == 0 else 1 - c) for k in line_order for q in range(2)] + [at(cc=1 - c)]
 
     def send(src, dst, ssem, rsem, dev):
         copy = pltpu.make_async_remote_copy(
@@ -154,69 +156,67 @@
             elif k == 2:
                 self.arrived(2, 3)
                 self.second(3)
+                self.go(15, 2, 0, self.far[2])
                 self.arrived(5, 9)
                 self.go(13, 3, 1, self.far[1])
                 self.arrived(6, 10)
                 self.go(14, 1, 1, self.far[1])
                 self.arrived(12)
-            elif k == 3:
-                self.arrived(7, 11)
-                self.go(15, 2, 3, self.far[0])
-                self.arrived(13, 14)
             else:
-                self.arrived(15)
+                self.arrived(7, 11, 13, 14, 15)
 
     half_a = Spread(
-        xpa, lambda d1, d2: lax.rem(y + d2, 4) * 4 + lax.rem(x + d1, 4), (xn, xq), (yn, yq), a_send, a_recv
+        xpa, lambda d1, d2: lax.rem(y + d2, 4) * 4 + lax.rem(x + d1, 4), (xn, xq), (yn, yq, at(yy=y + 2)), a_send, a_recv
     )
     half_b = Spread(
-        xpb, lambda d1, d2: lax.rem(y + d1, 4) * 4 + lax.rem(x + d2, 4), (yn, yq), (xn, xq), b_send, b_recv
+        xpb, lambda d1, d2: lax.rem(y + d1, 4) * 4 + lax.rem(x + d2, 4), (yn, yq), (xn, xq, at(xx=x + 2)), b_send, b_recv
     )
     ring_sent = {}
     parts = (pl.ds(0, 512), pl.ds(512, 512))
 
-    def ring(step, side, h):
-        owner = lax.rem(z + (8 - step if side == 0 else step), 8)
+    def ring(step, side, h, dist, dev):
+        owner = lax.rem(z + (8 - dist if side == 0 else dist), 8)
         key = step * 4 + side * 2 + h
-        ring_sent[key] = go(xl, (c, rows(owner), parts[h]), z_send, z_recv, key, (zn, zq)[side])
-
-    def ring_step(step, h):
+        ring_sent[key] = go(xl, (c, rows(owner), parts[h]), z_send, z_recv, key, dev)
+
+    def ring_hop(k, h):
         for side in range(2):
-            ring_sent[(step - 1) * 4 + side * 2 + h].wait_recv()
-            if step < 3 or side == h:
-                ring(step, side, h)
-
+            ring_sent[(k - 1) * 4 + side * 2 + h].wait_recv()
+            if k < 3:
+                ring(k, side, h, k, (zn, zq)[side])
+            if k == 2 and side == h:
+                ring(3, side, h, k, (at(zz=z + 2), at(zz=z + 6))[side])
+        if k == 3 and h == 1:
+            for key in (12, 15):
+                ring_sent[key].wait_recv()
+
+    half_a.start()
+    half_b.start()
+    for h in range(2):
+        for side in range(2):
+            ring(0, side, h, 0, (zn, zq)[side])
     for k in range(15):
         send(side_ref, side_p.at[me_p], sp_sems.at[0], sp_sems.at[1], plane_peers[k])
     for k in range(7):
         send(side_ref, side_l.at[z], sl_sems.at[0], sl_sems.at[1], line_same[k])
-    half_a.start()
-    half_b.start()
-    for h in range(2):
-        for side in range(2):
-            ring(0, side, h)
     side_p[me_p] = side_ref[...]
     side_l[z] = side_ref[...]
 
     def hop(k):
+        ring_hop(k, 0)
         half_a.hop(k)
+        ring_hop(k, 1)
         half_b.hop(k)
-        if k < 4:
-            ring_step(k, 0)
-            ring_step(k, 1)
-        else:
-            for key in (12, 15):
-                ring_sent[key].wait_recv()
 
     near = {0: ((0, 0),), 1: ((0, 1), (0, 3), (1, 0), (3, 0)),
             2: ((2, 0), (0, 2), (1, 1), (1, 3), (3, 1), (3, 3)),
-            3: ((2, 1), (2, 3), (1, 2), (3, 2)), 4: ((2, 2),)}
+            3: ((2, 1), (2, 3), (1, 2), (3, 2), (2, 2))}
 
     def plane_slots(k):
         return [lax.rem(y + dy, 4) * 4 + lax.rem(x + dx, 4) for dx, dy in near[k]]
 
     def line_slots(k):
-        return [lax.rem(z + d, 8) for d in ((k,) if k in (0, 4) else (k, 8 - k))]
+        return [lax.rem(z + d, 8) for d in {0: (0,), 1: (1, 7), 2: (2, 6), 3: (3, 5, 4)}[k]]
 
     def many(ref, count, sems, which):
         view = ref.at[pl.ds(0, count)]
@@ -298,10 +298,6 @@
         for k, chunk in enumerate(chunks):
             to, at_slot = pl.ds(k * CHUNK, CHUNK), rows(chunk[-1])
             chunk[4][at_slot, :] = sig[to, :] * wcol[to, :] - chunk[6][at_slot, :]
-        for slot in line:
-            for ref in (xl, hl, ol, il):
-                share(ref.at[c, rows(slot)])
-
     sub = lax.broadcasted_iota(jnp.int32, (8, 128), 0)
 
     def packed(lines, first=0):
@@ -317,13 +313,22 @@
         k = len(core_copies)
         core_copies.append(send(view, view, core_send.at[k], core_recv.at[k], partner))
 
+    def share_all(line):
+        for slot in line:
+            for ref in (xl, hl, ol, il):
+                share(ref.at[c, rows(slot)])
+
     loads[7].wait()
     hop(1)
     loads[8].wait()
-    batch(line_slots(0) + line_slots(1), plane_slots(0) + plane_slots(1), columns)
-    for k in (2, 3, 4):
+    line = line_slots(0) + line_slots(1)
+    batch(line, plane_slots(0) + plane_slots(1), columns)
+    for k in (2, 3):
         hop(k)
-        batch(line_slots(k), plane_slots(k), lambda: None)
+        share_all(line)
+        line = line_slots(k)
+        batch(line, plane_slots(k), lambda: None)
+    share_all(line)
 
     def as_lines(ref, count):
         return [jnp.sum(ref[pl.ds(b * 128, 128), :].T, axis=0, keepdims=True) for b in range(count)]
@@ -389,8 +394,8 @@
         return [jnp.zeros((1, 128), F32)] * 6 + [jnp.broadcast_to(m, (1, 128)), jnp.broadcast_to(n, (1, 128))]
 
     lines_p, part_l = products(r0p, r0l)
+    start_line(0, part_l)
     start_plane(0, packed(lines_p))
-    start_line(0, part_l)
     mine = pl.ds(pl.multiple_of(z * 128, 128), 128)
     for b in range(6):
         place = pl.ds((b % 3) * 128, 128)
@@ -400,8 +405,8 @@
     w0l = end_line(0) + DAMP * r0l
     m0, m1 = total_of(r0l * r0l), total_of(r0l * w0l)
     lines_p, part_l = products(w0p, w0l)
+    start_line(1, part_l)
     start_plane(1, packed(lines_p + scalars(m0, m1)[6:]))
-    start_line(1, part_l)
     got = end_plane(1)
     u0p = got + DAMP * w0p
     u0l = end_line(1) + DAMP * w0l
@@ -413,44 +418,57 @@
     start_plane(2, packed(scalars(m0, m1)))
     _, part_l = products(w1p, None)
     start_line(2, part_l)
+    basis = [
+        jnp.concatenate([vector[b : b + 1, :] for b in range(6)], axis=1) for vector in (r0l, r1l, w1l, w0l)
+    ]
+
+    def summed(which, turned_ref, right):
+        left = jnp.concatenate(
+            [turned_ref[pl.ds(pl.multiple_of(c * 32 + 64 * k, 32), 32), :] for k in range(2)], axis=0
+        )
+        scaled = [left * across for across in basis]
+        coarse = [value.astype(BF16) for value in scaled]
+        fine = [(value - part.astype(F32)).astype(BF16) for value, part in zip(scaled, coarse)]
+        stack = jnp.concatenate(coarse + fine, axis=0)
+        for n in range(4):
+            lanes = pl.ds(n * WIDE, WIDE)
+            got = dot(stack, right[:, :, lanes].reshape(SET, WIDE))
+            for k in range(4):
+                terms[which, k, :, lanes] = got[64 * k : 64 * k + 64] + got[256 + 64 * k : 320 + 64 * k]
+
+    summed(0, x_t, il)
     got = end_plane(2)
     u1l = end_line(2) + DAMP * w1l
     rr1, rw1 = got[6:7, :], got[7:8, :]
     be0 = rr1 / rr0
     al1 = rr1 / (rw1 - be0 * rr1 / al0)
-    d1 = r1l + be0 * r0l
     r2l = r1l - al1 * (w1l + be0 * w0l)
     w2l = w1l - al1 * (u1l + be0 * u0l)
     m0, m1 = total_of(r2l * r2l), total_of(r2l * w2l)
     start_plane(3, packed(scalars(m0, m1)))
+    summed(1, h_t, ol)
     got = end_plane(3)
     rr2, rw2 = got[6:7, :], got[7:8, :]
     be1 = rr2 / rr1
     al2 = rr2 / (rw2 - be1 * rr2 / al1)
-    sol = al0 * r0l + al1 * d1 + al2 * (r2l + be1 * d1)
-
-    across = jnp.concatenate([sol[b : b + 1, :] for b in range(6)], axis=1)
-
-    def summed(turned_ref, right):
-        left = jnp.concatenate(
-            [turned_ref[pl.ds(pl.multiple_of(c * 32 + 64 * k, 32), 32), :] for k in range(2)], axis=0
-        )
-        left = left * across
-        coarse = left.astype(BF16)
-        fine = (left - coarse.astype(F32)).astype(BF16)
-        both = dot(jnp.concatenate([coarse, fine], axis=0), right[...].reshape(SET, 1024))
-        return -LEARN * (both[0:64] + both[64:128])
-
-    one = summed(x_t, il)
-    two = summed(h_t, ol)
+    def combined(which, factors):
+        value = None
+        for k, factor in enumerate(factors):
+            term = terms[which, k] * jnp.concatenate([-LEARN * factor] * 8, axis=1)
+            value = term if value is None else value + term
+        return value
+
+    both = al1 + al2 * be1
+    one = combined(0, (al0 + both * be0, both + al2, -al2 * al1, -al2 * al1 * be0))
+    two = combined(1, (al0 + both * be0, both + al2, -al2 * al1, -al2 * al1 * be0))
     sub_wide = lax.broadcasted_iota(jnp.int32, (8, 1024), 0)
     for e in range(8):
         f, s = one[8 * e : 8 * e + 8], two[8 * e : 8 * e + 8]
         out_send[2 * e] = jnp.where(sub_wide < 4, f, pltpu.roll(s, 4, 0)).astype(BF16)
         out_send[2 * e + 1] = jnp.where(sub_wide < 4, pltpu.roll(f, 4, 0), s).astype(BF16)
-    for k in range(1, 16):
+    for k, peer in zip(plane_order, plane_peers):
         dest = lax.rem(y + k // 4, 4) * 4 + lax.rem(x + k % 4, 4)
-        send(out_send.at[dest], out_recv.at[me_p], out_sems.at[0], out_sems.at[1], plane_peers[k - 1])
+        send(out_send.at[dest], out_recv.at[me_p], out_sems.at[0], out_sems.at[1], peer)
     out_recv[me_p] = out_send[me_p]
     many(out_recv, 15, out_sems, 1)
     result = jnp.sum(out_recv[...].astype(F32), axis=0)
@@ -494,7 +512,7 @@
             pltpu.VMEM((HALF, 128), F32), pltpu.VMEM((HALF, 128), F32), pltpu.VMEM((HALF, 128), F32),
             pltpu.VMEM((SET, 128), F32), pltpu.VMEM((HALF, 128), F32),
             pltpu.VMEM((2, 8, 128), F32), pltpu.VMEM((128, SET), F32), pltpu.VMEM((128, SET), F32),
-            pltpu.VMEM((4, 16, 8, 128), F32), pltpu.VMEM((3, 16, 8, 128), F32),
+            pltpu.VMEM((2, 4, 64, 1024), F32), pltpu.VMEM((4, 16, 8, 128), F32), pltpu.VMEM((3, 16, 8, 128), F32),
             pltpu.VMEM((16, 8, 1024), BF16), pltpu.VMEM((16, 8, 1024), BF16),
             dma((9,)), dma((16,)), dma((16,)), dma((16,)), dma((16,)), dma((16,)), dma((16,)),
             dma((33,)), dma((33,)), dma((2,)), dma((2,)), dma((4, 2)), dma((3, 2)), dma((2,)),

time: 64.7 us -> 62.2 us (0.961)
  Pallas kernels: 63.2 us -> 60.7 us
    pallas_call x1, Pallas kernels: 63.2 us -> 60.7 us  [shards(): pl.pallas_call(step_kernel, out_shape=jax.ShapeDtypeStruct((4, 2048), F32...]
where the time goes in v4:
time: 62.2 us; the launch traced here: 62.1 us
  Pallas kernels  60.7 us (98%)
  local copies, waits for them, and re-layouts  1.38 us (2%)
    pallas_call x1, Pallas kernels, shards(): pl.pallas_call(step_kernel, out_shape=jax.ShapeDtypeStruct((4, 2048), F32...  60.7 us
    unnamed x1, local copies, waits for them, and re-layouts  1.38 us

profile of v4, /device:TPU:1, one launch (start us, length us, event | category | flops | bytes accessed | tf_op | source)
XLA Modules:
  0.0 62.1 jit_solution(14626624383195660313)
XLA Ops:
  0.0 60.7 %shard_map.73 = f32[4,2048]{1,0:T(4,128)} custom-call(bf16[48,1024]{1,0:T(8,128)(2,1)} %x_hbm.1, bf16[1024,1024]{1,0:T(8,128)(2,1)} %w1_hbm.1, bf16[1024,1024]{1,0:T(8,128)(2,1)} %w2_hbm.1, bf16[8,128]{1,0:T(8,128)(2,1)} %bitcast.4, f32[1,48]{1,0:T(1,128)} %bitcast.5, s32[1,48]{1,0:T(1,128)} %bitcast.6, s32[1,48]{1,0:T(1,128)} %bitcast.7), custom_call_target="tpu_custom_call" | custom-call | tf_op jit(solution)/shard_map/pallas_call | solution.py:493
  60.7 1.4 %copy.9 = f32[4,2048]{1,0:T(4,128)} copy(f32[4,2048]{1,0:T(4,128)} %shard_map.73) | data formatting | bytes 65536

commit v5 on v4

--- a/solution.py
+++ b/solution.py
@@ -393,6 +393,41 @@
     def scalars(m, n):
         return [jnp.zeros((1, 128), F32)] * 6 + [jnp.broadcast_to(m, (1, 128)), jnp.broadcast_to(n, (1, 128))]
 
+    def summed(which, at_term, vectors):
+        turned_ref, right = ((x_t, il), (h_t, ol))[which]
+        left = jnp.concatenate(
+            [turned_ref[pl.ds(pl.multiple_of(c * 32 + 64 * k, 32), 32), :] for k in range(2)], axis=0
+        )
+        basis = [jnp.concatenate([vector[b : b + 1, :] for b in range(6)], axis=1) for vector in vectors]
+        scaled = [left * across for across in basis]
+        coarse = [value.astype(BF16) for value in scaled]
+        fine = [(value - part.astype(F32)).astype(BF16) for value, part in zip(scaled, coarse)]
+        stack = jnp.concatenate(coarse + fine, axis=0)
+        half = 64 * len(vectors)
+        for n in range(4):
+            lanes = pl.ds(n * WIDE, WIDE)
+            found = dot(stack, right[:, :, lanes].reshape(SET, WIDE))
+            for k in range(len(vectors)):
+                near, far = found[64 * k : 64 * k + 64], found[half + 64 * k : half + 64 * k + 64]
+                terms[which, at_term + k, :, lanes] = near + far
+
+    sub_wide = lax.broadcasted_iota(jnp.int32, (8, 1024), 0)
+
+    def stage(slot, one, two):
+        for e in range(8):
+            f, s = one[8 * e : 8 * e + 8], two[8 * e : 8 * e + 8]
+            out_send[slot, 2 * e] = jnp.where(sub_wide < 4, f, pltpu.roll(s, 4, 0)).astype(BF16)
+            out_send[slot, 2 * e + 1] = jnp.where(sub_wide < 4, pltpu.roll(f, 4, 0), s).astype(BF16)
+        out_recv[slot, me_p] = out_send[slot, me_p]
+
+    def give(slot):
+        for k, peer in zip(plane_order, plane_peers):
+            dest = lax.rem(y + k // 4, 4) * 4 + lax.rem(x + k % 4, 4)
+            send(out_send.at[slot, dest], out_recv.at[slot, me_p], out_sems.at[slot, 0], out_sems.at[slot, 1], peer)
+
+    def whole(factor):
+        return jnp.concatenate([factor] * 8, axis=1)
+
     lines_p, part_l = products(r0p, r0l)
     start_line(0, part_l)
     start_plane(0, packed(lines_p))
@@ -401,12 +436,16 @@
         place = pl.ds((b % 3) * 128, 128)
         x_t[:, b * 128 : (b + 1) * 128] = xl[b // 3, place, mine].astype(F32).T
         h_t[:, b * 128 : (b + 1) * 128] = hl[b // 3, place, mine].astype(F32).T
+    summed(0, 0, (r0l,))
+    summed(1, 0, (r0l,))
+    stage(0, terms[0, 0], terms[1, 0])
     w0p = end_plane(0) + DAMP * r0p
     w0l = end_line(0) + DAMP * r0l
     m0, m1 = total_of(r0l * r0l), total_of(r0l * w0l)
     lines_p, part_l = products(w0p, w0l)
     start_line(1, part_l)
     start_plane(1, packed(lines_p + scalars(m0, m1)[6:]))
+    give(0)
     got = end_plane(1)
     u0p = got + DAMP * w0p
     u0l = end_line(1) + DAMP * w0l
@@ -418,25 +457,10 @@
     start_plane(2, packed(scalars(m0, m1)))
     _, part_l = products(w1p, None)
     start_line(2, part_l)
-    basis = [
-        jnp.concatenate([vector[b : b + 1, :] for b in range(6)], axis=1) for vector in (r0l, r1l, w1l, w0l)
-    ]
-
-    def summed(which, turned_ref, right):
-        left = jnp.concatenate(
-            [turned_ref[pl.ds(pl.multiple_of(c * 32 + 64 * k, 32), 32), :] for k in range(2)], axis=0
-        )
-        scaled = [left * across for across in basis]
-        coarse = [value.astype(BF16) for value in scaled]
-        fine = [(value - part.astype(F32)).astype(BF16) for value, part in zip(scaled, coarse)]
-        stack = jnp.concatenate(coarse + fine, axis=0)
-        for n in range(4):
-            lanes = pl.ds(n * WIDE, WIDE)
-            got = dot(stack, right[:, :, lanes].reshape(SET, WIDE))
-            for k in range(4):
-                terms[which, k, :, lanes] = got[64 * k : 64 * k + 64] + got[256 + 64 * k : 320 + 64 * k]
-
-    summed(0, x_t, il)
+    summed(0, 1, (r1l, w1l, w0l))
+    summed(1, 1, (r1l, w1l, w0l))
+    stage(1, terms[0, 1], terms[1, 1])
+    give(1)
     got = end_plane(2)
     u1l = end_line(2) + DAMP * w1l
     rr1, rw1 = got[6:7, :], got[7:8, :]
@@ -446,32 +470,20 @@
     w2l = w1l - al1 * (u1l + be0 * u0l)
     m0, m1 = total_of(r2l * r2l), total_of(r2l * w2l)
     start_plane(3, packed(scalars(m0, m1)))
-    summed(1, h_t, ol)
+    stage(2, *[
+        terms[k, 1] - whole(al1) * (terms[k, 2] + whole(be0) * terms[k, 3]) for k in range(2)
+    ])
+    give(2)
     got = end_plane(3)
     rr2, rw2 = got[6:7, :], got[7:8, :]
     be1 = rr2 / rr1
     al2 = rr2 / (rw2 - be1 * rr2 / al1)
-    def combined(which, factors):
-        value = None
-        for k, factor in enumerate(factors):
-            term = terms[which, k] * jnp.concatenate([-LEARN * factor] * 8, axis=1)
-            value = term if value is None else value + term
-        return value
-
     both = al1 + al2 * be1
-    one = combined(0, (al0 + both * be0, both + al2, -al2 * al1, -al2 * al1 * be0))
-    two = combined(1, (al0 + both * be0, both + al2, -al2 * al1, -al2 * al1 * be0))
-    sub_wide = lax.broadcasted_iota(jnp.int32, (8, 1024), 0)
-    for e in range(8):
-        f, s = one[8 * e : 8 * e + 8], two[8 * e : 8 * e + 8]
-        out_send[2 * e] = jnp.where(sub_wide < 4, f, pltpu.roll(s, 4, 0)).astype(BF16)
-        out_send[2 * e + 1] = jnp.where(sub_wide < 4, pltpu.roll(f, 4, 0), s).astype(BF16)
-    for k, peer in zip(plane_order, plane_peers):
-        dest = lax.rem(y + k // 4, 4) * 4 + lax.rem(x + k % 4, 4)
-        send(out_send.at[dest], out_recv.at[me_p], out_sems.at[0], out_sems.at[1], peer)
-    out_recv[me_p] = out_send[me_p]
-    many(out_recv, 15, out_sems, 1)
-    result = jnp.sum(out_recv[...].astype(F32), axis=0)
+    result = None
+    for slot, factor in enumerate((al0 + both * be0, both, al2)):
+        many(out_recv.at[slot], 15, out_sems.at[slot], 1)
+        term = jnp.sum(out_recv[slot].astype(F32), axis=0) * whole(-LEARN * factor)
+        result = term if result is None else result + term
     out_ref[:, 0:1024] = result[0:4]
     out_ref[:, 1024:2048] = result[4:8]
 
@@ -483,7 +495,8 @@
         many(plane_buf.at[k], 15, plane_sems.at[k], 0)
     for k in range(3):
         many(line_buf.at[k], 15, line_sems.at[k], 0)
-    many(out_send, 15, out_sems, 0)
+    for slot in range(3):
+        many(out_send.at[slot], 15, out_sems.at[slot], 0)
 
 
 def shards(inputs, first_weight, second_weight, readout, target, counts, views):
@@ -513,9 +526,9 @@
             pltpu.VMEM((SET, 128), F32), pltpu.VMEM((HALF, 128), F32),
             pltpu.VMEM((2, 8, 128), F32), pltpu.VMEM((128, SET), F32), pltpu.VMEM((128, SET), F32),
             pltpu.VMEM((2, 4, 64, 1024), F32), pltpu.VMEM((4, 16, 8, 128), F32), pltpu.VMEM((3, 16, 8, 128), F32),
-            pltpu.VMEM((16, 8, 1024), BF16), pltpu.VMEM((16, 8, 1024), BF16),
+            pltpu.VMEM((3, 16, 8, 1024), BF16), pltpu.VMEM((3, 16, 8, 1024), BF16),
             dma((9,)), dma((16,)), dma((16,)), dma((16,)), dma((16,)), dma((16,)), dma((16,)),
-            dma((33,)), dma((33,)), dma((2,)), dma((2,)), dma((4, 2)), dma((3, 2)), dma((2,)),
+            dma((33,)), dma((33,)), dma((2,)), dma((2,)), dma((4, 2)), dma((3, 2)), dma((3, 2)),
         ],
         compiler_params=pltpu.CompilerParams(
             collective_id=0, has_side_effects=True, vmem_limit_bytes=56 * 1024 * 1024

time: 62.2 us -> 59.8 us (0.961)
  Pallas kernels: 60.7 us -> 58.3 us
    pallas_call x1, Pallas kernels: 60.7 us -> 58.3 us  [shards(): pl.pallas_call(step_kernel, out_shape=jax.ShapeDtypeStruct((4, 2048), F32...]
where the time goes in v5:
time: 59.8 us; the launch traced here: 59.7 us
  Pallas kernels  58.3 us (97%)
  local copies, waits for them, and re-layouts  1.38 us (2%)
    pallas_call x1, Pallas kernels, shards(): pl.pallas_call(step_kernel, out_shape=jax.ShapeDtypeStruct((4, 2048), F32...  58.3 us
    unnamed x1, local copies, waits for them, and re-layouts  1.38 us

profile of v5, /device:TPU:1, one launch (start us, length us, event | category | flops | bytes accessed | tf_op | source)
XLA Modules:
  0.0 59.7 jit_solution(15481112013706057780)
XLA Ops:
  0.0 58.3 %shard_map.73 = f32[4,2048]{1,0:T(4,128)} custom-call(bf16[48,1024]{1,0:T(8,128)(2,1)} %x_hbm.1, bf16[1024,1024]{1,0:T(8,128)(2,1)} %w1_hbm.1, bf16[1024,1024]{1,0:T(8,128)(2,1)} %w2_hbm.1, bf16[8,128]{1,0:T(8,128)(2,1)} %bitcast.4, f32[1,48]{1,0:T(1,128)} %bitcast.5, s32[1,48]{1,0:T(1,128)} %bitcast.6, s32[1,48]{1,0:T(1,128)} %bitcast.7), custom_call_target="tpu_custom_call" | custom-call | tf_op jit(solution)/shard_map/pallas_call | solution.py:506
  58.3 1.4 %copy.9 = f32[4,2048]{1,0:T(4,128)} copy(f32[4,2048]{1,0:T(4,128)} %shard_map.73) | data formatting | bytes 65536

commit v6 on v5

--- a/solution.py
+++ b/solution.py
@@ -444,43 +444,55 @@
     m0, m1 = total_of(r0l * r0l), total_of(r0l * w0l)
     lines_p, part_l = products(w0p, w0l)
     start_line(1, part_l)
-    start_plane(1, packed(lines_p + scalars(m0, m1)[6:]))
+    first_lanes = lax.broadcasted_iota(jnp.int32, (1, 128), 1) < 64
+    start_plane(1, packed(lines_p + [
+        jnp.where(first_lanes, m0, total_of(w0l * w0l)), jnp.broadcast_to(m1, (1, 128))
+    ]))
     give(0)
     got = end_plane(1)
     u0p = got + DAMP * w0p
     u0l = end_line(1) + DAMP * w0l
-    rr0, rw0 = got[6:7, :], got[7:8, :]
+    rr0, rw0 = jnp.broadcast_to(got[6:7, 0:1], (1, 128)), got[7:8, :]
+    w0w0 = jnp.broadcast_to(got[6:7, 64:65], (1, 128))
     al0 = rr0 / rw0
     r1l, w1l = r0l - al0 * w0l, w0l - al0 * u0l
     w1p = w0p - al0 * u0p
     m0, m1 = total_of(r1l * r1l), total_of(r1l * w1l)
-    start_plane(2, packed(scalars(m0, m1)))
+    near0 = al0 * al0 * w0w0 / rr0 - 1.0
+    e1l = r1l + near0 * r0l
+    start_plane(2, packed([
+        jnp.broadcast_to(value, (1, 128)) for value in (m0, m1, total_of(w1l * w1l), total_of(w1l * w0l))
+    ]))
     _, part_l = products(w1p, None)
     start_line(2, part_l)
-    summed(0, 1, (r1l, w1l, w0l))
-    summed(1, 1, (r1l, w1l, w0l))
+    summed(0, 1, (e1l, w1l, w0l))
+    summed(1, 1, (e1l, w1l, w0l))
     stage(1, terms[0, 1], terms[1, 1])
     give(1)
     got = end_plane(2)
     u1l = end_line(2) + DAMP * w1l
-    rr1, rw1 = got[6:7, :], got[7:8, :]
+    rr1, rw1, w1w1, w1w0 = [got[k : k + 1, :] for k in range(4)]
     be0 = rr1 / rr0
     al1 = rr1 / (rw1 - be0 * rr1 / al0)
     r2l = r1l - al1 * (w1l + be0 * w0l)
     w2l = w1l - al1 * (u1l + be0 * u0l)
     m0, m1 = total_of(r2l * r2l), total_of(r2l * w2l)
     start_plane(3, packed(scalars(m0, m1)))
+    near1 = al1 * al1 * (w1w1 + 2.0 * be0 * w1w0 + be0 * be0 * w0w0) / rr1 - 1.0
+    left_over = be0 - near0
     stage(2, *[
-        terms[k, 1] - whole(al1) * (terms[k, 2] + whole(be0) * terms[k, 3]) for k in range(2)
+        whole(1.0 + near1) * terms[k, 1] + whole(near1 * left_over - near0) * terms[k, 0]
+        - whole(al1) * (terms[k, 2] + whole(be0) * terms[k, 3])
+        for k in range(2)
     ])
     give(2)
     got = end_plane(3)
     rr2, rw2 = got[6:7, :], got[7:8, :]
     be1 = rr2 / rr1
     al2 = rr2 / (rw2 - be1 * rr2 / al1)
-    both = al1 + al2 * be1
+    both = al1 + al2 * (be1 - near1)
     result = None
-    for slot, factor in enumerate((al0 + both * be0, both, al2)):
+    for slot, factor in enumerate((al0 + both * left_over, both, al2)):
         many(out_recv.at[slot], 15, out_sems.at[slot], 1)
         term = jnp.sum(out_recv[slot].astype(F32), axis=0) * whole(-LEARN * factor)
         result = term if result is None else result + term

time: 59.8 us -> 59.8 us (level)
  no operation moved by 1% of the time
where the time goes in v6:
time: 59.8 us; the launch traced here: 59.7 us
  Pallas kernels  58.3 us (97%)
  local copies, waits for them, and re-layouts  1.38 us (2%)
    pallas_call x1, Pallas kernels, shards(): pl.pallas_call(step_kernel, out_shape=jax.ShapeDtypeStruct((4, 2048), F32...  58.3 us
    unnamed x1, local copies, waits for them, and re-layouts  1.38 us

profile of v6, /device:TPU:1, one launch (start us, length us, event | category | flops | bytes accessed | tf_op | source)
XLA Modules:
  0.0 59.7 jit_solution(14307440902707780757)
XLA Ops:
  0.0 58.3 %shard_map.73 = f32[4,2048]{1,0:T(4,128)} custom-call(bf16[48,1024]{1,0:T(8,128)(2,1)} %x_hbm.1, bf16[1024,1024]{1,0:T(8,128)(2,1)} %w1_hbm.1, bf16[1024,1024]{1,0:T(8,128)(2,1)} %w2_hbm.1, bf16[8,128]{1,0:T(8,128)(2,1)} %bitcast.4, f32[1,48]{1,0:T(1,128)} %bitcast.5, s32[1,48]{1,0:T(1,128)} %bitcast.6, s32[1,48]{1,0:T(1,128)} %bitcast.7), custom_call_target="tpu_custom_call" | custom-call | tf_op jit(solution)/shard_map/pallas_call | solution.py:518
  58.3 1.4 %copy.9 = f32[4,2048]{1,0:T(4,128)} copy(f32[4,2048]{1,0:T(4,128)} %shard_map.73) | data formatting | bytes 65536
